TPU v7x, 128 devices: a whole 4x4x4 slice. The times are simulated.
128 devices in a mesh: grp: 4 (over y), row: 32 (over z, x, core).
Axes of the slice: x: 4, y: 4, z: 4, core: 2. Of those that a mesh axis runs over, the one named last changes fastest.
Arguments:
- tiles: bfloat16 [4, 32, 32, 256, 256], P('grp', 'row'), may hold values from -0.046875 to 0.046875
- tile_rows: int32 [4, 32, 32], P('grp', 'row'), may hold values from 0 to 3, as said below
- tile_cols: int32 [4, 32, 32], P('grp', 'row'), may hold values from 0 to 31, as said below
- live_tiles: int32 [4, 32], P('grp', 'row'), may hold values from 16 to 32, as said below
- dual_shift: float32 [32768], P('row'), may hold values from 0.5 to 2
- start_block: float32 [32, 32768], P(None, 'row'), may hold values from -6 to 6
Outputs:
- projections: float32 [4, 32, 128], replicated
- factors: float32 [4, 32, 32], replicated
- next_block: float32 [32, 32768], P(None, 'row')
Inputs may be any that keep to these rules, and one draw needn't show every extreme that they name: `tile_rows`: the tile slots of one device sit at distinct positions (block row, column block), padding slots included. `tile_cols`: column block j of group g is global block column (j // 1) * 4 + g * 1 + j % 1. Slots from live_tiles on are padding with arbitrary values; in every draw some device has all 32 slots live.
All inputs are finite; a program needn't handle non-finite values.
Results may differ from a plain program's by a relative error of at most 0.013.
Values may be sent and summed in bfloat16 or wider, within the bound.
A program may use at most 64 MiB of HBM per device.

v0:
```python
import functools

import jax
import jax.numpy as jnp
from jax import lax
from jax.experimental import pallas as pl
from jax.experimental.pallas import tpu as pltpu
from jax.sharding import PartitionSpec as P

ITERS = 4
MESH = pl.DeviceIdType.MESH
HIGH = lax.Precision.HIGHEST
NT = (((1,), (1,)), ((), ()))


def dot_nt(a, b):
    return lax.dot_general(a, b, NT, precision=HIGH, preferred_element_type=jnp.float32)


def dot_nn(a, b):
    return jnp.dot(a, b, precision=HIGH, preferred_element_type=jnp.float32)


def factor_and_inverse(gram):
    n = gram.shape[0]
    row = lax.broadcasted_iota(jnp.int32, (n, 2 * n), 0)
    lane = lax.broadcasted_iota(jnp.int32, (n, 2 * n), 1)
    work = jnp.concatenate([gram, jnp.where(row == lane, 1.0, 0.0)[:, :n]], axis=1)
    lower = jnp.zeros((n, n), jnp.float32)
    pivots = jnp.zeros((n, 2 * n), jnp.float32)
    for k in range(n):
        column = jnp.broadcast_to(work[:, k : k + 1], (n, 2 * n))
        pivot_row = work[k : k + 1, :]
        pivot = column[k : k + 1, :]
        scale = 1.0 / pivot
        below = jnp.where(row > k, column, 0.0)
        lower = jnp.where((lane[:, :n] == k) & (row[:, :n] >= k), column[:, :n] * lax.rsqrt(pivot[:, :n]), lower)
        pivots = jnp.where(row == k, pivot, pivots)
        work = work - below * (pivot_row * scale)
    inverse = (work * lax.rsqrt(pivots))[:, n:]
    return lower, inverse


def kernel(
    steps, group_count, owner_count,
    start_ref, shift_ref, place_ref, tiles_hbm,
    proj_ref, fac_ref, next_ref,
    tiles_ref, dense, gathered, own, back_out, back_in, direct_out, direct_in,
    pair_out, pair_in, dots_pair, dots_grp, dots_row, basis, images, current, last, tile_sem,
    gather_row_send, gather_row_recv, gather_grp_send, gather_grp_recv,
    back_send, back_recv, direct_send, direct_recv,
    dgrp_send, dgrp_recv, drow_send, drow_recv, last_send, last_recv,
    relay_send, pair_send, pair_recv, dpair_send, dpair_recv,
):
    g = lax.axis_index("grp")
    r = lax.axis_index("row")
    width = start_ref.shape[0]
    row_count = start_ref.shape[1]
    part = row_count // group_count
    edge = tiles_ref.shape[1]
    owned = row_count // edge
    per_part = part // edge
    chips = owner_count // 2
    chip, core = r // 2, lax.rem(r, 2)
    partner = chip * 2 + 1 - core
    chip_peers = [lax.rem(chip + d, chips) for d in range(1, chips)]
    row_peers = [peer * 2 + core for peer in chip_peers] + [partner]
    grp_peers = [lax.rem(g + d, group_count) for d in range(1, group_count)]

    load = pltpu.make_async_copy(tiles_hbm, tiles_ref, tile_sem)
    load.start()
    barrier = pltpu.get_barrier_semaphore()
    for peer in row_peers:
        pl.semaphore_signal(barrier, inc=1, device_id=(g, peer), device_id_type=MESH)
    for peer in grp_peers:
        pl.semaphore_signal(barrier, inc=1, device_id=(peer, r), device_id_type=MESH)
    pl.semaphore_wait(barrier, len(row_peers) + len(grp_peers))

    def to_row(peer, src, dst, send, recv):
        return pltpu.make_async_remote_copy(
            src_ref=src, dst_ref=dst, send_sem=send, recv_sem=recv,
            device_id=(g, peer), device_id_type=MESH,
        )

    def to_grp(peer, src, dst, send, recv):
        return pltpu.make_async_remote_copy(
            src_ref=src, dst_ref=dst, send_sem=send, recv_sem=recv,
            device_id=(peer, r), device_id_type=MESH,
        )

    def send_grp_dots(value):
        dots_grp[g] = value
        sends = []
        for peer in grp_peers:
            copy = to_grp(peer, dots_grp.at[g], dots_grp.at[g], dgrp_send.at[peer], dgrp_recv.at[g])
            copy.start()
            sends.append(copy)
        return sends

    def take_grp_dots():
        for peer in grp_peers:
            to_grp(peer, dots_grp.at[peer], dots_grp.at[peer], dgrp_send.at[peer], dgrp_recv.at[peer]).wait_recv()
        total = dots_grp[0]
        for index in range(1, group_count):
            total = total + dots_grp[index]
        return total

    def send_pair_dots(half, value):
        dots_pair[half, core] = value
        copy = to_row(
            partner, dots_pair.at[half, core], dots_pair.at[half, core], dpair_send, dpair_recv.at[half]
        )
        copy.start()
        return [copy]

    def send_row_dots(half):
        to_row(
            partner, dots_pair.at[half, 1 - core], dots_pair.at[half, 1 - core], dpair_send, dpair_recv.at[half]
        ).wait_recv()
        dots_row[half, chip] = dots_pair[half, 0] + dots_pair[half, 1]
        sends = []
        for peer in chip_peers:
            copy = to_row(
                peer * 2 + core, dots_row.at[half, chip], dots_row.at[half, chip],
                drow_send.at[peer], drow_recv.at[half, chip],
            )
            copy.start()
            sends.append(copy)
        return sends

    def take_row_dots(half):
        for peer in chip_peers:
            to_row(
                peer * 2 + core, dots_row.at[half, peer], dots_row.at[half, peer],
                drow_send.at[peer], drow_recv.at[half, peer],
            ).wait_recv()
        total = dots_row[half, 0]
        for index in range(1, chips):
            total = total + dots_row[half, index]
        return total

    fold = 128 // width

    def pack(square):
        height = width // fold
        return jnp.concatenate([square[i * height : (i + 1) * height] for i in range(fold)], axis=1)

    def unpack(packed):
        return jnp.concatenate([packed[:, i * width : (i + 1) * width] for i in range(fold)], axis=0)

    total_cols = steps * width

    def local_dots(block):
        dots = dot_nt(block, jnp.concatenate([basis[...], block], axis=0))
        return jnp.concatenate([dots[:, :total_cols], pack(dots[:, total_cols:])], axis=0)

    def finish_dots(summed):
        first = summed[:width]
        gram = unpack(summed[width:]) - dot_nt(first, first)
        lower, inverse = factor_and_inverse(gram)
        return first, lower, inverse

    basis[...] = jnp.zeros_like(basis)
    images[...] = jnp.zeros_like(images)
    mine = pl.ds(pl.multiple_of(g * part, part), part)
    current[...] = start_ref[:, mine]
    load.wait()
    for j in range(owner_count * per_part):
        for i in range(owned):
            slot = place_ref[i * owner_count * per_part + j]
            keep = jnp.where(slot > 0, 1.0, 0.0).astype(jnp.bfloat16)
            tile = tiles_ref[jnp.maximum(slot - 1, 0)]
            dense[
                j // per_part,
                i * edge : (i + 1) * edge,
                (j % per_part) * edge : (j % per_part + 1) * edge,
            ] = tile * keep

    def both(value):
        return value[:width] + value[width:]

    def step_body(step, carry):
        half = lax.rem(step, 2)
        block = current[...]
        high = block.astype(jnp.bfloat16)
        rest = (block - high.astype(jnp.float32)).astype(jnp.bfloat16)
        split = jnp.concatenate([high, rest], axis=0)
        own[g] = split
        gathered[half, r] = split
        sends = []
        for peer in grp_peers:
            copy = to_grp(peer, own.at[g], own.at[g], gather_grp_send.at[peer], gather_grp_recv.at[g])
            copy.start()
            sends.append(copy)
        for peer in row_peers:
            copy = to_row(
                peer, gathered.at[half, r], gathered.at[half, r],
                gather_row_send.at[peer], gather_row_recv.at[half, r],
            )
            copy.start()
            sends.append(copy)
        sends += send_grp_dots(local_dots(block))
        for peer in grp_peers:
            to_grp(peer, own.at[peer], own.at[peer], gather_grp_send.at[peer], gather_grp_recv.at[peer]).wait_recv()
        full = jnp.concatenate([own[i] for i in range(group_count)], axis=1)
        for peer in chip_peers + [chip]:
            pair_out[peer] = both(
                jnp.dot(full, dense[peer * 2 + 1 - core], preferred_element_type=jnp.float32)
            )
            copy = to_row(
                partner, pair_out.at[peer], pair_in.at[half, peer], pair_send.at[peer], pair_recv.at[half, peer]
            )
            copy.start()
            sends.append(copy)
        kept = [
            both(jnp.dot(full, dense[peer * 2 + core], preferred_element_type=jnp.float32))
            for peer in chip_peers
        ]

        def take_pair(peer):
            to_row(
                partner, pair_out.at[peer], pair_in.at[half, peer], pair_send.at[peer], pair_recv.at[half, peer]
            ).wait_recv()
            return pair_in[half, peer]

        for peer, value in zip(chip_peers, kept):
            back_out[peer] = value + take_pair(peer)
            copy = to_row(
                peer * 2 + core, back_out.at[peer], back_in.at[half, chip],
                back_send.at[peer], back_recv.at[half, chip],
            )
            copy.start()
            sends.append(copy)
        sends += send_pair_dots(half, take_grp_dots())
        for peer in chip_peers:
            slot = peer * 2 + core
            to_row(
                slot, gathered.at[half, slot], gathered.at[half, slot],
                gather_row_send.at[slot], gather_row_recv.at[half, slot],
            ).wait_recv()
            copy = to_row(
                partner, gathered.at[half, slot], gathered.at[half, slot],
                relay_send.at[peer], gather_row_recv.at[half, slot],
            )
            copy.start()
            sends.append(copy)
        sends += send_row_dots(half)
        total = both(jnp.dot(full, dense[r], preferred_element_type=jnp.float32)) + take_pair(chip)
        for peer in chip_peers + [chip]:
            slot = peer * 2 + 1 - core
            to_row(
                partner, gathered.at[half, slot], gathered.at[half, slot],
                relay_send.at[peer], gather_row_recv.at[half, slot],
            ).wait_recv()

        def forward(quarter):
            rows = pl.ds(pl.multiple_of(quarter * part, part), part)
            value = jnp.zeros((2 * width, part), jnp.float32)
            for j in range(owner_count):
                value = value + lax.dot_general(
                    gathered[half, j], dense[j, rows, :], NT, preferred_element_type=jnp.float32
                )
            return both(value)

        for peer in grp_peers:
            direct_out[peer] = forward(peer)
            copy = to_grp(peer, direct_out.at[peer], direct_in.at[g], direct_send.at[peer], direct_recv.at[g])
            copy.start()
            sends.append(copy)
        total = total + forward(g)

        first, lower, inverse = finish_dots(take_row_dots(half))
        last_step = jnp.maximum(step - 1, 0)
        proj_ref[last_step] = first
        fac_ref[last_step] = lower
        now = dot_nn(inverse, block - dot_nn(first, basis[...]))

        for peer in chip_peers:
            to_row(
                peer * 2 + core, back_out.at[peer], back_in.at[half, peer],
                back_send.at[peer], back_recv.at[half, peer],
            ).wait_recv()
            total = total + back_in[half, peer]
        for peer in grp_peers:
            to_grp(peer, direct_out.at[peer], direct_in.at[peer], direct_send.at[peer], direct_recv.at[peer]).wait_recv()
            total = total + direct_in[peer]
        image = dot_nn(inverse, 0.5 * total - dot_nn(first, images[...]))
        place = pl.ds(pl.multiple_of(step * width, width), width)
        basis[place, :] = now
        images[place, :] = image
        current[...] = image - now * shift_ref[:, mine]
        for copy in sends:
            copy.wait_send()
        return carry

    lax.fori_loop(0, steps, step_body, 0)

    block = current[...]
    sends = send_grp_dots(local_dots(block))
    sends += send_pair_dots(steps % 2, take_grp_dots())
    sends += send_row_dots(steps % 2)
    block_parts = take_row_dots(steps % 2)
    first, lower, inverse = finish_dots(block_parts)
    proj_ref[steps - 1] = first
    fac_ref[steps - 1] = lower
    last[g] = dot_nn(inverse, block - dot_nn(first, basis[...]))
    for peer in grp_peers:
        copy = to_grp(peer, last.at[g], last.at[g], last_send.at[peer], last_recv.at[g])
        copy.start()
        sends.append(copy)
    for peer in grp_peers:
        to_grp(peer, last.at[peer], last.at[peer], last_send.at[peer], last_recv.at[peer]).wait_recv()
    for index in range(group_count):
        next_ref[:, index * part : (index + 1) * part] = last[index]
    for copy in sends:
        copy.wait_send()


def hand_on(proj_in, fac_in, next_in, proj_ref, fac_ref, next_ref):
    proj_ref[...] = proj_in[...]
    fac_ref[...] = fac_in[...]
    next_ref[...] = next_in[...]


def per_device(tiles, tile_rows, tile_cols, live_tiles, dual_shift, start_block):
    matrix = tiles[0, 0]
    tile_count, edge = matrix.shape[0], matrix.shape[1]
    width, row_count = start_block.shape
    group_count = lax.axis_size("grp")
    owner_count = lax.axis_size("row")
    owned = row_count // edge
    part = row_count // group_count
    columns = part // edge * owner_count
    total_cols = ITERS * width
    order = jnp.arange(tile_count, dtype=jnp.int32)
    position = tile_rows[0, 0] * columns + tile_cols[0, 0]
    here = (position[None, :] == jnp.arange(owned * columns, dtype=jnp.int32)[:, None]) & (
        order < live_tiles[0, 0]
    )[None, :]
    place = jnp.sum(jnp.where(here, order[None, :] + 1, 0), axis=1).astype(jnp.int32)

    vmem = pl.BlockSpec(memory_space=pltpu.VMEM)
    smem = pl.BlockSpec(memory_space=pltpu.SMEM)
    dma = pltpu.SemaphoreType.DMA
    packed = width + width * width // 128
    grp_sem = dma((group_count,))
    row_sem = dma((owner_count,))
    row_pair = dma((2, owner_count))
    shapes = (
            jax.ShapeDtypeStruct((ITERS, width, total_cols), jnp.float32),
            jax.ShapeDtypeStruct((ITERS, width, width), jnp.float32),
            jax.ShapeDtypeStruct((width, row_count), jnp.float32),
    )
    outs = pl.pallas_call(
        functools.partial(kernel, ITERS, group_count, owner_count),
        out_shape=shapes,
        in_specs=[vmem, vmem, smem, pl.BlockSpec(memory_space=pl.ANY)],
        out_specs=(vmem, vmem, vmem),
        scratch_shapes=[
            pltpu.VMEM(matrix.shape, jnp.bfloat16),
            pltpu.VMEM((owner_count, row_count, part), jnp.bfloat16),
            pltpu.VMEM((2, owner_count, 2 * width, part), jnp.bfloat16),
            pltpu.VMEM((group_count, 2 * width, part), jnp.bfloat16),
            pltpu.VMEM((owner_count // 2, width, part), jnp.float32),
            pltpu.VMEM((2, owner_count // 2, width, part), jnp.float32),
            pltpu.VMEM((group_count, width, part), jnp.float32),
            pltpu.VMEM((group_count, width, part), jnp.float32),
            pltpu.VMEM((owner_count // 2, width, part), jnp.float32),
            pltpu.VMEM((2, owner_count // 2, width, part), jnp.float32),
            pltpu.VMEM((2, 2, packed, total_cols), jnp.float32),
            pltpu.VMEM((group_count, packed, total_cols), jnp.float32),
            pltpu.VMEM((2, owner_count // 2, packed, total_cols), jnp.float32),
            pltpu.VMEM((total_cols, part), jnp.float32),
            pltpu.VMEM((total_cols, part), jnp.float32),
            pltpu.VMEM((width, part), jnp.float32),
            pltpu.VMEM((group_count, width, part), jnp.float32),
            pltpu.SemaphoreType.DMA,
            row_sem, row_pair, grp_sem, grp_sem,
            row_sem, row_pair, grp_sem, grp_sem,
            grp_sem, grp_sem, row_sem, row_pair, grp_sem, grp_sem,
            row_sem, row_sem, row_pair, dma, dma((2,)),
        ],
        compiler_params=pltpu.CompilerParams(
            collective_id=0, has_side_effects=True, vmem_limit_bytes=60 * 1024 * 1024
        ),
    )(start_block, dual_shift[None, :], place, matrix)
    return pl.pallas_call(hand_on, out_shape=shapes, in_specs=[vmem] * 3, out_specs=(vmem,) * 3)(*outs)


def solution(mesh):
    in_specs = (
        P("grp", "row", None, None, None),
        P("grp", "row", None),
        P("grp", "row", None),
        P("grp", "row"),
        P("row"),
        P(None, "row"),
    )
    out_specs = (P(), P(), P(None, "row"))
    return jax.shard_map(
        per_device, mesh=mesh, in_specs=in_specs, out_specs=out_specs, check_vma=False
    )
```

profile of v0, /device:TPU:1, one launch (start us, length us, event | category | flops | bytes accessed | tf_op | source)
XLA Modules:
  0.0 138.9 jit_solution(9598349861876766291)
XLA Ops:
  1.3 0.7 add_bitcast_fusion
  2.0 0.6 select_reduce_fusion.place_ref
  2.6 134.6 %shard_map.85 = (f32[4,32,128]{2,1,0:T(8,128)}, f32[4,32,32]{2,1,0:T(8,128)}, f32[32,1024]{1,0:T(8,128)}) custom-call(f32[32,1024]{1,0:T(8,128)} %start_ref.1, f32[1,1024]{1,0:T(1,128)} %bitcast.7, s32[128]{0:T(128)} %select_reduce_fusion.place_ref, bf16[32,256,256]{2,1,0:T(8,128)(2,1)} %bitcast.6), custom_call_target="tpu_custom_call" | custom-call | tf_op jit(solution)/shard_map/pallas_call | solution.py:354
  137.2 1.7 %shard_map.86 = (f32[4,32,128]{2,1,0:T(8,128)}, f32[4,32,32]{2,1,0:T(8,128)}, f32[32,1024]{1,0:T(8,128)}) custom-call(f32[4,32,128]{2,1,0:T(8,128)} %get-tuple-element.6.proj_in, f32[4,32,32]{2,1,0:T(8,128)} %get-tuple-element.7.fac_in, f32[32,1024]{1,0:T(8,128)} %get-tuple-element.8.next_in), custom_call_target="tpu_custom_call" | custom-call | tf_op jit(solution)/shard_map/pallas_call | solution.py:387
  (2 shorter events, 0.0 us)
where the time goes:
time: 139 us
  Pallas kernels  136 us (98%)
    pallas_call x1, Pallas kernels, per_device(): pl.pallas_call(functools.partial(kernel, ITERS, group_count, owner_count)...  135 us

commit v1 on v0

--- a/solution.py
+++ b/solution.py
@@ -11,6 +11,7 @@
 MESH = pl.DeviceIdType.MESH
 HIGH = lax.Precision.HIGHEST
 NT = (((1,), (1,)), ((), ()))
+MIDDLE = 1.25
 
 
 def dot_nt(a, b):
@@ -43,10 +44,10 @@
 
 def kernel(
     steps, group_count, owner_count,
-    start_ref, shift_ref, place_ref, tiles_hbm,
+    start_ref, shift_ref, rows_ref, cols_ref, place_ref, tiles_hbm,
     proj_ref, fac_ref, next_ref,
-    tiles_ref, dense, gathered, own, back_out, back_in, direct_out, direct_in,
-    pair_out, pair_in, dots_pair, dots_grp, dots_row, basis, images, current, last, tile_sem,
+    tiles_ref, products, gathered, stage, own, back_out, back_in, direct, direct_out, direct_in,
+    pair_out, pair_in, dots_pair, dots_grp, dots_row, basis, images, current, operand, coef, last, tile_sem,
     gather_row_send, gather_row_recv, gather_grp_send, gather_grp_recv,
     back_send, back_recv, direct_send, direct_recv,
     dgrp_send, dgrp_recv, drow_send, drow_recv, last_send, last_recv,
@@ -57,9 +58,8 @@
     width = start_ref.shape[0]
     row_count = start_ref.shape[1]
     part = row_count // group_count
-    edge = tiles_ref.shape[1]
-    owned = row_count // edge
-    per_part = part // edge
+    tile_count = tiles_ref.shape[0]
+    owned = row_count // tiles_ref.shape[1]
     chips = owner_count // 2
     chip, core = r // 2, lax.rem(r, 2)
     partner = chip * 2 + 1 - core
@@ -162,31 +162,26 @@
 
     basis[...] = jnp.zeros_like(basis)
     images[...] = jnp.zeros_like(images)
+    coef[...] = jnp.zeros_like(coef)
+    products[tile_count] = jnp.zeros((width, part), jnp.float32)
     mine = pl.ds(pl.multiple_of(g * part, part), part)
     current[...] = start_ref[:, mine]
+    operand[...] = start_ref[:, mine].astype(jnp.bfloat16)
+    shift = shift_ref[:, mine]
     load.wait()
-    for j in range(owner_count * per_part):
-        for i in range(owned):
-            slot = place_ref[i * owner_count * per_part + j]
-            keep = jnp.where(slot > 0, 1.0, 0.0).astype(jnp.bfloat16)
-            tile = tiles_ref[jnp.maximum(slot - 1, 0)]
-            dense[
-                j // per_part,
-                i * edge : (i + 1) * edge,
-                (j % per_part) * edge : (j % per_part + 1) * edge,
-            ] = tile * keep
-
-    def both(value):
-        return value[:width] + value[width:]
+
+    def back_product(slot):
+        value = products[place_ref[slot]]
+        for i in range(1, owned):
+            value = value + products[place_ref[i * owner_count + slot]]
+        return value
 
     def step_body(step, carry):
         half = lax.rem(step, 2)
         block = current[...]
-        high = block.astype(jnp.bfloat16)
-        rest = (block - high.astype(jnp.float32)).astype(jnp.bfloat16)
-        split = jnp.concatenate([high, rest], axis=0)
-        own[g] = split
-        gathered[half, r] = split
+        own[g] = operand[...]
+        gathered[half, r] = operand[...]
+        stage[r] = operand[...]
         sends = []
         for peer in grp_peers:
             copy = to_grp(peer, own.at[g], own.at[g], gather_grp_send.at[peer], gather_grp_recv.at[g])
@@ -202,36 +197,33 @@
         sends += send_grp_dots(local_dots(block))
         for peer in grp_peers:
             to_grp(peer, own.at[peer], own.at[peer], gather_grp_send.at[peer], gather_grp_recv.at[peer]).wait_recv()
-        full = jnp.concatenate([own[i] for i in range(group_count)], axis=1)
+        for k in range(tile_count):
+            products[k] = jnp.dot(own[rows_ref[k]], tiles_ref[k], preferred_element_type=jnp.float32)
         for peer in chip_peers + [chip]:
-            pair_out[peer] = both(
-                jnp.dot(full, dense[peer * 2 + 1 - core], preferred_element_type=jnp.float32)
-            )
+            pair_out[peer] = back_product(peer * 2 + 1 - core).astype(jnp.bfloat16)
             copy = to_row(
                 partner, pair_out.at[peer], pair_in.at[half, peer], pair_send.at[peer], pair_recv.at[half, peer]
             )
             copy.start()
             sends.append(copy)
-        kept = [
-            both(jnp.dot(full, dense[peer * 2 + core], preferred_element_type=jnp.float32))
-            for peer in chip_peers
-        ]
 
         def take_pair(peer):
             to_row(
                 partner, pair_out.at[peer], pair_in.at[half, peer], pair_send.at[peer], pair_recv.at[half, peer]
             ).wait_recv()
-            return pair_in[half, peer]
-
-        for peer, value in zip(chip_peers, kept):
-            back_out[peer] = value + take_pair(peer)
+            return pair_in[half, peer].astype(jnp.float32)
+
+        sends += send_pair_dots(half, take_grp_dots())
+        for peer in chip_peers:
+            back_out[peer] = (back_product(peer * 2 + core) + take_pair(peer)).astype(jnp.bfloat16)
             copy = to_row(
                 peer * 2 + core, back_out.at[peer], back_in.at[half, chip],
                 back_send.at[peer], back_recv.at[half, chip],
             )
             copy.start()
             sends.append(copy)
-        sends += send_pair_dots(half, take_grp_dots())
+        total = back_product(r) + take_pair(chip)
+        sends += send_row_dots(half)
         for peer in chip_peers:
             slot = peer * 2 + core
             to_row(
@@ -244,51 +236,64 @@
             )
             copy.start()
             sends.append(copy)
-        sends += send_row_dots(half)
-        total = both(jnp.dot(full, dense[r], preferred_element_type=jnp.float32)) + take_pair(chip)
+            stage[slot] = gathered[half, slot]
         for peer in chip_peers + [chip]:
             slot = peer * 2 + 1 - core
             to_row(
                 partner, gathered.at[half, slot], gathered.at[half, slot],
                 relay_send.at[peer], gather_row_recv.at[half, slot],
             ).wait_recv()
-
-        def forward(quarter):
-            rows = pl.ds(pl.multiple_of(quarter * part, part), part)
-            value = jnp.zeros((2 * width, part), jnp.float32)
-            for j in range(owner_count):
-                value = value + lax.dot_general(
-                    gathered[half, j], dense[j, rows, :], NT, preferred_element_type=jnp.float32
-                )
-            return both(value)
-
-        for peer in grp_peers:
-            direct_out[peer] = forward(peer)
+            stage[slot] = gathered[half, slot]
+
+        forward = jnp.zeros((part, owned * width), jnp.float32)
+        for k in range(tile_count):
+            vector = stage[cols_ref[k]]
+            row = rows_ref[tile_count + k]
+            spread = jnp.concatenate(
+                [vector * jnp.where(row == i, 1.0, 0.0).astype(jnp.bfloat16) for i in range(owned)], axis=0
+            )
+            forward = forward + lax.dot_general(tiles_ref[k], spread, NT, preferred_element_type=jnp.float32)
+        forward = forward.T
+        for i in range(owned):
+            direct[i] = forward[i * width : (i + 1) * width]
+            direct_out[i] = forward[i * width : (i + 1) * width].astype(jnp.bfloat16)
+        for peer in grp_peers:
             copy = to_grp(peer, direct_out.at[peer], direct_in.at[g], direct_send.at[peer], direct_recv.at[g])
             copy.start()
             sends.append(copy)
-        total = total + forward(g)
+        total = total + direct[g]
 
         first, lower, inverse = finish_dots(take_row_dots(half))
         last_step = jnp.maximum(step - 1, 0)
         proj_ref[last_step] = first
         fac_ref[last_step] = lower
         now = dot_nn(inverse, block - dot_nn(first, basis[...]))
+        rest = dot_nn(coef[...] - first, images[...])
+        before = pl.ds(pl.multiple_of(last_step * width, width), width)
+        place = pl.ds(pl.multiple_of(step * width, width), width)
+        follow = jnp.where(step > 0, lower, 0.0).T
+        ahead = now * (MIDDLE - shift) - dot_nn(follow, basis[before, :])
+        lane = lax.broadcasted_iota(jnp.int32, (width, total_cols), 1)
+        sub = lax.broadcasted_iota(jnp.int32, (width, total_cols), 0)
+        wide = jnp.concatenate([follow] * (total_cols // width), axis=1)
+        coef[...] = jnp.where(lane == step * width + sub, -MIDDLE, 0.0) + jnp.where(
+            (lane >= last_step * width) & (lane < last_step * width + width), wide, 0.0
+        )
 
         for peer in chip_peers:
             to_row(
                 peer * 2 + core, back_out.at[peer], back_in.at[half, peer],
                 back_send.at[peer], back_recv.at[half, peer],
             ).wait_recv()
-            total = total + back_in[half, peer]
+            total = total + back_in[half, peer].astype(jnp.float32)
         for peer in grp_peers:
             to_grp(peer, direct_out.at[peer], direct_in.at[peer], direct_send.at[peer], direct_recv.at[peer]).wait_recv()
-            total = total + direct_in[peer]
-        image = dot_nn(inverse, 0.5 * total - dot_nn(first, images[...]))
-        place = pl.ds(pl.multiple_of(step * width, width), width)
+            total = total + direct_in[peer].astype(jnp.float32)
+        image = dot_nn(inverse, 0.5 * total + rest)
         basis[place, :] = now
         images[place, :] = image
-        current[...] = image - now * shift_ref[:, mine]
+        current[...] = image - now * shift
+        operand[...] = (image + ahead).astype(jnp.bfloat16)
         for copy in sends:
             copy.wait_send()
         return carry
@@ -337,7 +342,9 @@
     here = (position[None, :] == jnp.arange(owned * columns, dtype=jnp.int32)[:, None]) & (
         order < live_tiles[0, 0]
     )[None, :]
-    place = jnp.sum(jnp.where(here, order[None, :] + 1, 0), axis=1).astype(jnp.int32)
+    place = tile_count - jnp.sum(jnp.where(here, tile_count - order[None, :], 0), axis=1).astype(jnp.int32)
+    rows = jnp.concatenate([tile_rows[0, 0], jnp.where(order < live_tiles[0, 0], tile_rows[0, 0], owned)])
+    cols = tile_cols[0, 0]
 
     vmem = pl.BlockSpec(memory_space=pltpu.VMEM)
     smem = pl.BlockSpec(memory_space=pltpu.SMEM)
@@ -354,25 +361,29 @@
     outs = pl.pallas_call(
         functools.partial(kernel, ITERS, group_count, owner_count),
         out_shape=shapes,
-        in_specs=[vmem, vmem, smem, pl.BlockSpec(memory_space=pl.ANY)],
+        in_specs=[vmem, vmem, smem, smem, smem, pl.BlockSpec(memory_space=pl.ANY)],
         out_specs=(vmem, vmem, vmem),
         scratch_shapes=[
             pltpu.VMEM(matrix.shape, jnp.bfloat16),
-            pltpu.VMEM((owner_count, row_count, part), jnp.bfloat16),
-            pltpu.VMEM((2, owner_count, 2 * width, part), jnp.bfloat16),
-            pltpu.VMEM((group_count, 2 * width, part), jnp.bfloat16),
-            pltpu.VMEM((owner_count // 2, width, part), jnp.float32),
-            pltpu.VMEM((2, owner_count // 2, width, part), jnp.float32),
+            pltpu.VMEM((tile_count + 1, width, part), jnp.float32),
+            pltpu.VMEM((2, owner_count, width, part), jnp.bfloat16),
+            pltpu.VMEM((owner_count, width, part), jnp.bfloat16),
+            pltpu.VMEM((group_count, width, part), jnp.bfloat16),
+            pltpu.VMEM((owner_count // 2, width, part), jnp.bfloat16),
+            pltpu.VMEM((2, owner_count // 2, width, part), jnp.bfloat16),
             pltpu.VMEM((group_count, width, part), jnp.float32),
-            pltpu.VMEM((group_count, width, part), jnp.float32),
-            pltpu.VMEM((owner_count // 2, width, part), jnp.float32),
-            pltpu.VMEM((2, owner_count // 2, width, part), jnp.float32),
+            pltpu.VMEM((group_count, width, part), jnp.bfloat16),
+            pltpu.VMEM((group_count, width, part), jnp.bfloat16),
+            pltpu.VMEM((owner_count // 2, width, part), jnp.bfloat16),
+            pltpu.VMEM((2, owner_count // 2, width, part), jnp.bfloat16),
             pltpu.VMEM((2, 2, packed, total_cols), jnp.float32),
             pltpu.VMEM((group_count, packed, total_cols), jnp.float32),
             pltpu.VMEM((2, owner_count // 2, packed, total_cols), jnp.float32),
             pltpu.VMEM((total_cols, part), jnp.float32),
             pltpu.VMEM((total_cols, part), jnp.float32),
             pltpu.VMEM((width, part), jnp.float32),
+            pltpu.VMEM((width, part), jnp.bfloat16),
+            pltpu.VMEM((width, total_cols), jnp.float32),
             pltpu.VMEM((group_count, width, part), jnp.float32),
             pltpu.SemaphoreType.DMA,
             row_sem, row_pair, grp_sem, grp_sem,
@@ -383,7 +394,7 @@
         compiler_params=pltpu.CompilerParams(
             collective_id=0, has_side_effects=True, vmem_limit_bytes=60 * 1024 * 1024
         ),
-    )(start_block, dual_shift[None, :], place, matrix)
+    )(start_block, dual_shift[None, :], rows, cols, place, matrix)
     return pl.pallas_call(hand_on, out_shape=shapes, in_specs=[vmem] * 3, out_specs=(vmem,) * 3)(*outs)
 
 

time: 139 us -> 112 us (0.81)
  Pallas kernels: 136 us -> 108 us
    pallas_call x1, Pallas kernels: 135 us -> 106 us  [per_device(): pl.pallas_call(functools.partial(kernel, ITERS, group_count, owner_count)...]
where the time goes in v1:
time: 112 us
  Pallas kernels  108 us (96%)
  other arithmetic  2.54 us (2%)
  between operations  1.29 us (1%)
    pallas_call x1, Pallas kernels, per_device(): pl.pallas_call(functools.partial(kernel, ITERS, group_count, owner_count)...  106 us

profile of v1, /device:TPU:1, one launch (start us, length us, event | category | flops | bytes accessed | tf_op | source)
XLA Modules:
  0.0 111.8 jit_solution(3702069327809964762)
XLA Ops:
  1.3 0.7 multiply_add_fusion
  2.0 0.1 select_reduce_fusion
  2.1 0.5 broadcast_subtract_fusion.place_ref
  2.6 1.2 %pad_add_fusion.rows_ref = s32[64]{0:T(128)} fusion(s32[32]{0:T(128)S(1)} %get-tuple-element.10, s32[32]{0:T(128)} %bitcast.13), kind=kLoop, calls=%fused_computation.3 | loop fusion | flops 64 | bytes 512 | tf_op jit(solution)/shard_map/concatenate | solution.py:346
  3.8 106.3 %shard_map.85 = (f32[4,32,128]{2,1,0:T(8,128)}, f32[4,32,32]{2,1,0:T(8,128)}, f32[32,1024]{1,0:T(8,128)}) custom-call(f32[32,1024]{1,0:T(8,128)} %start_ref.1, f32[1,1024]{1,0:T(1,128)} %bitcast.11, s32[64]{0:T(128)} %pad_add_fusion.rows_ref, s32[32]{0:T(128)} %bitcast.12, s32[128]{0:T(128)} %broadcast_subtract_fusion.place_ref, bf16[32,256,256]{2,1,0:T(8,128)(2,1)} %bitcast.10), custom_call_target="tpu_custom_call" | custom-call | tf_op jit(solution)/shard_map/pallas_call | solution.py:361
  110.2 1.7 %shard_map.86 = (f32[4,32,128]{2,1,0:T(8,128)}, f32[4,32,32]{2,1,0:T(8,128)}, f32[32,1024]{1,0:T(8,128)}) custom-call(f32[4,32,128]{2,1,0:T(8,128)} %get-tuple-element.6.proj_in, f32[4,32,32]{2,1,0:T(8,128)} %get-tuple-element.7.fac_in, f32[32,1024]{1,0:T(8,128)} %get-tuple-element.8.next_in), custom_call_target="tpu_custom_call" | custom-call | tf_op jit(solution)/shard_map/pallas_call | solution.py:398
  (1 shorter events, 0.0 us)

commit v2 on v1

v2 whole, which is shorter than its diff:
```python
import functools

import jax
import jax.numpy as jnp
from jax import lax
from jax.experimental import pallas as pl
from jax.experimental.pallas import tpu as pltpu
from jax.sharding import PartitionSpec as P

ITERS = 4
MESH = pl.DeviceIdType.MESH
HIGH = lax.Precision.HIGHEST
NT = (((1,), (1,)), ((), ()))
MIDDLE = 1.25
PANEL = 8


def dot_nt(a, b):
    return lax.dot_general(a, b, NT, precision=HIGH, preferred_element_type=jnp.float32)


def dot_nn(a, b):
    return jnp.dot(a, b, precision=HIGH, preferred_element_type=jnp.float32)


def factor_and_inverse(gram):
    n = gram.shape[0]
    row = lax.broadcasted_iota(jnp.int32, (n, 2 * n), 0)
    lane = lax.broadcasted_iota(jnp.int32, (n, 2 * n), 1)
    work = jnp.concatenate([gram, jnp.where(row == lane, 1.0, 0.0)[:, :n]], axis=1)
    lower = jnp.zeros((n, 2 * n), jnp.float32)
    scales = jnp.zeros((n, 2 * n), jnp.float32)
    for start in range(0, n, PANEL):
        columns = [jnp.broadcast_to(work[:, k : k + 1], (n, 2 * n)) for k in range(start, start + PANEL)]
        rows = [work[k : k + 1, :] for k in range(start, start + PANEL)]
        update = jnp.zeros((n, 2 * n), jnp.float32)
        for i in range(PANEL):
            k = start + i
            scale = lax.rsqrt(columns[i][k : k + 1, :])
            column = columns[i] * scale
            pivot_row = rows[i] * scale
            for later in range(i + 1, PANEL):
                weight = column[start + later : start + later + 1, :]
                columns[later] = columns[later] - column * weight
                rows[later] = rows[later] - pivot_row * weight
            update = update + jnp.where(row > k, column, 0.0) * pivot_row
            lower = jnp.where((lane == k) & (row >= k), column, lower)
            scales = jnp.where(row == k, scale, scales)
        work = work - update
    inverse = (work * scales)[:, n:]
    return lower[:, :n], inverse


def kernel(
    steps, group_count, owner_count,
    start_ref, shift_ref, rows_ref, cols_ref, live_ref, tiles_hbm,
    proj_ref, fac_ref, next_ref,
    tiles_ref, products, gathered, stage, history, own, own_history, back_out, back_in, direct, direct_out, direct_in,
    pair_out, pair_in, dots_grp, basis, images, current, operand, coef, transform, place_vector, place_ref, tile_sem, place_sem,
    gather_row_send, gather_row_recv, gather_grp_send, gather_grp_recv,
    back_send, back_recv, direct_send, direct_recv,
    dgrp_send, dgrp_recv, relay_send, pair_send, pair_recv,
):
    g = lax.axis_index("grp")
    r = lax.axis_index("row")
    width = start_ref.shape[0]
    row_count = start_ref.shape[1]
    part = row_count // group_count
    tile_count = tiles_ref.shape[0]
    owned = row_count // tiles_ref.shape[1]
    chips = owner_count // 2
    chip, core = r // 2, lax.rem(r, 2)
    partner = chip * 2 + 1 - core
    chip_peers = [lax.rem(chip + d, chips) for d in range(1, chips)]
    row_peers = [peer * 2 + core for peer in chip_peers] + [partner]
    grp_peers = [lax.rem(g + d, group_count) for d in range(1, group_count)]
    total_cols = steps * width

    load = pltpu.make_async_copy(tiles_hbm, tiles_ref, tile_sem)
    load.start()
    barrier = pltpu.get_barrier_semaphore()
    for peer in row_peers:
        pl.semaphore_signal(barrier, inc=1, device_id=(g, peer), device_id_type=MESH)
    for peer in grp_peers:
        pl.semaphore_signal(barrier, inc=1, device_id=(peer, r), device_id_type=MESH)

    lanes = lax.broadcasted_iota(jnp.int32, place_vector.shape, 1)
    place = jnp.full(place_vector.shape, tile_count, jnp.int32)
    for k in range(tile_count):
        position = jnp.where(k < live_ref[0, 0], rows_ref[k] * owner_count + cols_ref[k], -1)
        place = jnp.where(lanes == position, k, place)
    place_vector[...] = place
    place_copy = pltpu.make_async_copy(place_vector, place_ref, place_sem)
    place_copy.start()
    basis[...] = jnp.zeros_like(basis)
    images[...] = jnp.zeros_like(images)
    coef[...] = jnp.zeros_like(coef)
    transform[...] = jnp.zeros_like(transform)
    history[...] = jnp.zeros_like(history)
    products[tile_count] = jnp.zeros((width, part), jnp.float32)
    mine = pl.ds(pl.multiple_of(g * part, part), part)
    current[...] = start_ref[:, mine]
    operand[...] = start_ref[:, mine].astype(jnp.bfloat16)
    shift = shift_ref[:, mine]
    place_copy.wait()
    pl.semaphore_wait(barrier, len(row_peers) + len(grp_peers))

    def to_row(peer, src, dst, send, recv):
        return pltpu.make_async_remote_copy(
            src_ref=src, dst_ref=dst, send_sem=send, recv_sem=recv,
            device_id=(g, peer), device_id_type=MESH,
        )

    def to_grp(peer, src, dst, send, recv):
        return pltpu.make_async_remote_copy(
            src_ref=src, dst_ref=dst, send_sem=send, recv_sem=recv,
            device_id=(peer, r), device_id_type=MESH,
        )

    def send_vectors(half):
        own[g] = operand[...]
        gathered[half, r] = operand[...]
        stage[r] = operand[...]
        sends = []
        for peer in row_peers:
            copy = to_row(
                peer, gathered.at[half, r], gathered.at[half, r],
                gather_row_send.at[peer], gather_row_recv.at[half, r],
            )
            copy.start()
            sends.append(copy)
        for peer in grp_peers:
            copy = to_grp(peer, own.at[g], own.at[g], gather_grp_send.at[peer], gather_grp_recv.at[g])
            copy.start()
            sends.append(copy)
        return sends

    def take_own(step):
        for peer in grp_peers:
            to_grp(peer, own.at[peer], own.at[peer], gather_grp_send.at[peer], gather_grp_recv.at[peer]).wait_recv()
        rows = pl.ds(pl.multiple_of(step * width, width), width)
        for i in range(group_count):
            own_history[rows, i * part : (i + 1) * part] = own[i]

    def relay_vectors(half):
        sends = []
        for peer in chip_peers:
            slot = peer * 2 + core
            to_row(
                slot, gathered.at[half, slot], gathered.at[half, slot],
                gather_row_send.at[slot], gather_row_recv.at[half, slot],
            ).wait_recv()
            copy = to_row(
                partner, gathered.at[half, slot], gathered.at[half, slot],
                relay_send.at[peer], gather_row_recv.at[half, slot],
            )
            copy.start()
            sends.append(copy)
            stage[slot] = gathered[half, slot]
        return sends

    def take_relayed(half):
        for peer in [chip] + chip_peers:
            slot = peer * 2 + 1 - core
            to_row(
                partner, gathered.at[half, slot], gathered.at[half, slot],
                relay_send.at[peer], gather_row_recv.at[half, slot],
            ).wait_recv()
            stage[slot] = gathered[half, slot]

    fold = 128 // width

    def pack(square):
        height = width // fold
        return jnp.concatenate([square[i * height : (i + 1) * height] for i in range(fold)], axis=1)

    def unpack(packed):
        return jnp.concatenate([packed[:, i * width : (i + 1) * width] for i in range(fold)], axis=0)

    def send_dots(half):
        dots = jnp.zeros((total_cols + width, width), jnp.float32)
        for slot in range(owner_count):
            vector = stage[slot]
            dots = dots + lax.dot_general(
                jnp.concatenate([history[slot], vector], axis=0), vector, NT, preferred_element_type=jnp.float32
            )
        dots = dots.T
        dots_grp[half, g] = jnp.concatenate([dots[:, :total_cols], pack(dots[:, total_cols:])], axis=0)
        sends = []
        for peer in grp_peers:
            copy = to_grp(
                peer, dots_grp.at[half, g], dots_grp.at[half, g], dgrp_send.at[peer], dgrp_recv.at[half, g]
            )
            copy.start()
            sends.append(copy)
        return sends

    def take_dots(half):
        for peer in grp_peers:
            to_grp(
                peer, dots_grp.at[half, peer], dots_grp.at[half, peer], dgrp_send.at[peer], dgrp_recv.at[half, peer]
            ).wait_recv()
        summed = dots_grp[half, 0]
        for index in range(1, group_count):
            summed = summed + dots_grp[half, index]
        return summed

    def finish_dots(summed):
        cross = dot_nt(summed[:width], transform[...])
        gram = unpack(summed[width:]) - dot_nt(cross, cross)
        lower, inverse = factor_and_inverse(gram)
        return cross, lower, inverse

    def back_product(slot):
        value = products[place_ref[0, slot]]
        for i in range(1, owned):
            value = value + products[place_ref[0, i * owner_count + slot]]
        return value

    lane = lax.broadcasted_iota(jnp.int32, (width, total_cols), 1)
    sub = lax.broadcasted_iota(jnp.int32, (width, total_cols), 0)

    def step_body(step, carry):
        half = lax.rem(step, 2)
        sends = send_vectors(half)
        take_own(step)
        for k in range(tile_count):
            products[k] = jnp.dot(own[rows_ref[k]], tiles_ref[k], preferred_element_type=jnp.float32)
        for peer in chip_peers + [chip]:
            pair_out[peer] = back_product(peer * 2 + 1 - core).astype(jnp.bfloat16)
            copy = to_row(
                partner, pair_out.at[peer], pair_in.at[half, peer], pair_send.at[peer], pair_recv.at[half, peer]
            )
            copy.start()
            sends.append(copy)

        def take_pair(peer):
            to_row(
                partner, pair_out.at[peer], pair_in.at[half, peer], pair_send.at[peer], pair_recv.at[half, peer]
            ).wait_recv()
            return pair_in[half, peer].astype(jnp.float32)

        sends += relay_vectors(half)
        for peer in chip_peers:
            back_out[peer] = (back_product(peer * 2 + core) + take_pair(peer)).astype(jnp.bfloat16)
            copy = to_row(
                peer * 2 + core, back_out.at[peer], back_in.at[half, chip],
                back_send.at[peer], back_recv.at[half, chip],
            )
            copy.start()
            sends.append(copy)
        total = back_product(r) + take_pair(chip)
        take_relayed(half)
        sends += send_dots(half)
        forward = jnp.zeros((part, owned * width), jnp.float32)
        for k in range(tile_count):
            vector = stage[cols_ref[k]]
            row = jnp.where(k < live_ref[0, 0], rows_ref[k], owned)
            spread = jnp.concatenate(
                [vector * jnp.where(row == i, 1.0, 0.0).astype(jnp.bfloat16) for i in range(owned)], axis=0
            )
            forward = forward + lax.dot_general(tiles_ref[k], spread, NT, preferred_element_type=jnp.float32)
        forward = forward.T
        for i in range(owned):
            direct[i] = forward[i * width : (i + 1) * width]
            direct_out[i] = forward[i * width : (i + 1) * width].astype(jnp.bfloat16)
        for peer in grp_peers:
            copy = to_grp(peer, direct_out.at[peer], direct_in.at[g], direct_send.at[peer], direct_recv.at[g])
            copy.start()
            sends.append(copy)
        total = total + direct[g]
        place = pl.ds(pl.multiple_of(step * width, width), width)
        for slot in range(owner_count):
            history[slot, place, :] = stage[slot]

        summed = take_dots(half)
        cross, lower, inverse = finish_dots(summed)
        last_step = jnp.maximum(step - 1, 0)
        proj_ref[last_step] = cross + coef[...]
        fac_ref[last_step] = lower
        now = dot_nn(inverse, current[...] - dot_nn(cross, basis[...]))
        rest = dot_nn(cross, images[...])
        transform[place, :] = dot_nn(
            inverse, jnp.where(lane == step * width + sub, 1.0, 0.0) - dot_nn(cross, transform[...])
        )
        before = pl.ds(pl.multiple_of(last_step * width, width), width)
        follow = jnp.where(step > 0, lower, 0.0).T
        ahead = now * (MIDDLE - shift) - dot_nn(follow, basis[before, :])
        wide = jnp.concatenate([follow] * (total_cols // width), axis=1)
        coef[...] = jnp.where(lane == step * width + sub, -MIDDLE, 0.0) + jnp.where(
            (lane >= last_step * width) & (lane < last_step * width + width), wide, 0.0
        )
        basis[place, :] = now

        for peer in chip_peers:
            to_row(
                peer * 2 + core, back_out.at[peer], back_in.at[half, peer],
                back_send.at[peer], back_recv.at[half, peer],
            ).wait_recv()
            total = total + back_in[half, peer].astype(jnp.float32)
        for peer in grp_peers:
            to_grp(peer, direct_out.at[peer], direct_in.at[peer], direct_send.at[peer], direct_recv.at[peer]).wait_recv()
            total = total + direct_in[peer].astype(jnp.float32)
        image = dot_nn(inverse, 0.5 * total - rest)
        images[place, :] = image
        current[...] = image + ahead
        operand[...] = (image + ahead).astype(jnp.bfloat16)
        for copy in sends:
            copy.wait_send()
        return carry

    load.wait()
    lax.fori_loop(0, steps, step_body, 0)

    half = steps % 2
    sends = send_vectors(half)
    sends += relay_vectors(half)
    take_relayed(half)
    sends += send_dots(half)
    take_own(steps)
    summed = take_dots(half)
    cross, lower, inverse = finish_dots(summed)
    proj_ref[steps - 1] = cross + coef[...]
    fac_ref[steps - 1] = lower
    combine = jnp.concatenate([-dot_nn(inverse, dot_nn(cross, transform[...])), inverse], axis=1)
    high = combine.astype(jnp.bfloat16)
    low = (combine - high.astype(jnp.float32)).astype(jnp.bfloat16)
    both = jnp.dot(jnp.concatenate([high, low], axis=0), own_history[...], preferred_element_type=jnp.float32)
    next_ref[...] = both[:width] + both[width:]
    for copy in sends:
        copy.wait_send()


def hand_on(proj_in, fac_in, next_in, proj_ref, fac_ref, next_ref):
    proj_ref[...] = proj_in[...]
    fac_ref[...] = fac_in[...]
    next_ref[...] = next_in[...]


def per_device(tiles, tile_rows, tile_cols, live_tiles, dual_shift, start_block):
    matrix = tiles[0, 0]
    tile_count, edge = matrix.shape[0], matrix.shape[1]
    width, row_count = start_block.shape
    group_count = lax.axis_size("grp")
    owner_count = lax.axis_size("row")
    owned = row_count // edge
    part = row_count // group_count
    total_cols = ITERS * width
    vmem = pl.BlockSpec(memory_space=pltpu.VMEM)
    smem = pl.BlockSpec(memory_space=pltpu.SMEM)
    dma = pltpu.SemaphoreType.DMA
    packed = width + width * width // 128
    grp_sem = dma((group_count,))
    row_sem = dma((owner_count,))
    row_pair = dma((2, owner_count))
    shapes = (
            jax.ShapeDtypeStruct((ITERS, width, total_cols), jnp.float32),
            jax.ShapeDtypeStruct((ITERS, width, width), jnp.float32),
            jax.ShapeDtypeStruct((width, row_count), jnp.float32),
    )
    outs = pl.pallas_call(
        functools.partial(kernel, ITERS, group_count, owner_count),
        out_shape=shapes,
        in_specs=[vmem, vmem, smem, smem, smem, pl.BlockSpec(memory_space=pltpu.HBM)],
        out_specs=(vmem, vmem, vmem),
        scratch_shapes=[
            pltpu.VMEM(matrix.shape, jnp.bfloat16),
            pltpu.VMEM((tile_count + 1, width, part), jnp.float32),
            pltpu.VMEM((2, owner_count, width, part), jnp.bfloat16),
            pltpu.VMEM((owner_count, width, part), jnp.bfloat16),
            pltpu.VMEM((owner_count, total_cols, part), jnp.bfloat16),
            pltpu.VMEM((group_count, width, part), jnp.bfloat16),
            pltpu.VMEM((total_cols + width, row_count), jnp.bfloat16),
            pltpu.VMEM((owner_count // 2, width, part), jnp.bfloat16),
            pltpu.VMEM((2, owner_count // 2, width, part), jnp.bfloat16),
            pltpu.VMEM((group_count, width, part), jnp.float32),
            pltpu.VMEM((group_count, width, part), jnp.bfloat16),
            pltpu.VMEM((group_count, width, part), jnp.bfloat16),
            pltpu.VMEM((owner_count // 2, width, part), jnp.bfloat16),
            pltpu.VMEM((2, owner_count // 2, width, part), jnp.bfloat16),
            pltpu.VMEM((2, group_count, packed, total_cols), jnp.float32),
            pltpu.VMEM((total_cols, part), jnp.float32),
            pltpu.VMEM((total_cols, part), jnp.float32),
            pltpu.VMEM((width, part), jnp.float32),
            pltpu.VMEM((width, part), jnp.bfloat16),
            pltpu.VMEM((width, total_cols), jnp.float32),
            pltpu.VMEM((total_cols, total_cols), jnp.float32),
            pltpu.VMEM((8, owned * owner_count), jnp.int32),
            pltpu.SMEM((8, owned * owner_count), jnp.int32),
            dma, dma,
            row_sem, row_pair, grp_sem, grp_sem,
            row_sem, row_pair, grp_sem, grp_sem,
            grp_sem, dma((2, group_count)), row_sem, row_sem, row_pair,
        ],
        compiler_params=pltpu.CompilerParams(
            collective_id=0, has_side_effects=True, vmem_limit_bytes=24 * 1024 * 1024
        ),
    )(start_block, dual_shift[None, :], tile_rows[0, 0], tile_cols[0, 0], live_tiles, matrix)
    return pl.pallas_call(hand_on, out_shape=shapes, in_specs=[vmem] * 3, out_specs=(vmem,) * 3)(*outs)


def solution(mesh):
    in_specs = (
        P("grp", "row", None, None, None),
        P("grp", "row", None),
        P("grp", "row", None),
        P("grp", "row"),
        P("row"),
        P(None, "row"),
    )
    out_specs = (P(), P(), P(None, "row"))
    return jax.shard_map(
        per_device, mesh=mesh, in_specs=in_specs, out_specs=out_specs, check_vma=False
    )
```

time: 112 us -> 95.1 us (0.85)
  Pallas kernels: 108 us -> 86.5 us
  local copies, waits for them, and re-layouts: 0 us -> 6.96 us
  other arithmetic: 2.54 us -> 0 us
    pallas_call x1, Pallas kernels: 106 us -> 84.9 us  [per_device(): pl.pallas_call(functools.partial(kernel, ITERS, group_count, owner_count)...]
    unnamed x0 -> x16, local copies, waits for them, and re-layouts: none -> 6.96 us
    concatenate x1 -> x0, other arithmetic: 1.24 us -> none  [per_device(): jnp.concatenate([tile_rows[0, 0], jnp.where(order < live_tiles[0, 0], til...]
where the time goes in v2:
time: 95.1 us; the launch traced here: 94.8 us
  Pallas kernels  86.5 us (91%)
  local copies, waits for them, and re-layouts  6.96 us (7%)
  between operations  1.31 us (1%)
    pallas_call x1, Pallas kernels, per_device(): pl.pallas_call(functools.partial(kernel, ITERS, group_count, owner_count)...  84.9 us
    unnamed x16, local copies, waits for them, and re-layouts  6.96 us

profile of v2, /device:TPU:1, one launch (start us, length us, event | category | flops | bytes accessed | tf_op | source)
XLA Modules:
  0.0 94.8 jit_solution(2347649404882770490)
XLA Ops:
  1.3 0.0 copy-start
  1.3 2.2 %copy-done = bf16[1,1,32,256,256]{4,3,2,1,0:T(8,128)(2,1)S(1)} copy-done((bf16[1,1,32,256,256]{4,3,2,1,0:T(8,128)(2,1)S(1)}, bf16[1,1,32,256,256]{4,3,2,1,0:T(8,128)(2,1)}, u32[]{:S(2)}) %copy-start) | copy-done | bytes 4194328
  3.5 0.0 copy-start.1
  3.5 0.9 copy-done.1
  4.4 0.0 copy-start.5
  4.4 0.7 copy-done.5
  5.1 0.0 copy-start.6
  5.1 0.7 copy-done.6
  5.7 0.0 copy-start.7
  5.7 0.7 copy-done.7
  6.4 84.9 %shard_map.85 = (f32[4,32,128]{2,1,0:T(8,128)S(1)}, f32[4,32,32]{2,1,0:T(8,128)S(1)}, f32[32,1024]{1,0:T(8,128)S(1)}) custom-call(f32[32,1024]{1,0:T(8,128)S(1)} %copy-done.1, f32[1,1024]{1,0:T(1,128)S(1)} %bitcast.5, s32[32]{0:T(128)S(1)} %bitcast.6, s32[32]{0:T(128)S(1)} %bitcast.7, s32[1,1]{1,0:T(1,128)S(6)} %copy.9.live_ref, ...), custom_call_target="tpu_custom_call" | custom-call | tf_op jit(solution)/shard_map/pallas_call | solution.py:361
  91.2 0.0 copy-start.2
  91.3 0.6 copy-done.2
  91.9 0.0 copy-start.3
  91.9 0.6 copy-done.3
  92.5 0.0 copy-start.4
  92.5 0.6 copy-done.4
  93.1 1.7 %shard_map.86 = (f32[4,32,128]{2,1,0:T(8,128)}, f32[4,32,32]{2,1,0:T(8,128)}, f32[32,1024]{1,0:T(8,128)}) custom-call(f32[4,32,128]{2,1,0:T(8,128)} %copy-done.3, f32[4,32,32]{2,1,0:T(8,128)} %copy-done.4, f32[32,1024]{1,0:T(8,128)} %copy-done.2), custom_call_target="tpu_custom_call" | custom-call | tf_op jit(solution)/shard_map/pallas_call | solution.py:399
Async XLA Ops:
  1.3 2.2 %copy-start = (bf16[1,1,32,256,256]{4,3,2,1,0:T(8,128)(2,1)S(1)}, bf16[1,1,32,256,256]{4,3,2,1,0:T(8,128)(2,1)}, u32[]{:S(2)}) copy-start(bf16[1,1,32,256,256]{4,3,2,1,0:T(8,128)(2,1)} %param.6) | copy-start | bytes 12582916
  3.5 0.9 copy-start.1
  4.4 0.7 copy-start.5
  5.1 0.7 copy-start.6
  5.7 0.7 copy-start.7
  91.2 0.7 copy-start.2
  91.9 0.6 copy-start.3
  92.5 0.6 copy-start.4

commit v3 on v2

v3 whole, which is shorter than its diff:
```python
import functools

import jax
import jax.numpy as jnp
from jax import lax
from jax.experimental import pallas as pl
from jax.experimental.pallas import tpu as pltpu
from jax.sharding import PartitionSpec as P

ITERS = 4
MESH = pl.DeviceIdType.MESH
HIGH = lax.Precision.HIGHEST
NT = (((1,), (1,)), ((), ()))
MIDDLE = 1.25
PANEL = 8
SIDE = 4


def dot_nt(a, b):
    return lax.dot_general(a, b, NT, precision=HIGH, preferred_element_type=jnp.float32)


def dot_nn(a, b):
    return jnp.dot(a, b, precision=HIGH, preferred_element_type=jnp.float32)


def factor_and_inverse(gram):
    n = gram.shape[0]
    row = lax.broadcasted_iota(jnp.int32, (n, 2 * n), 0)
    lane = lax.broadcasted_iota(jnp.int32, (n, 2 * n), 1)
    work = jnp.concatenate([gram, jnp.where(row == lane, 1.0, 0.0)[:, :n]], axis=1)
    lower = jnp.zeros((n, 2 * n), jnp.float32)
    scales = jnp.zeros((n, 2 * n), jnp.float32)
    for start in range(0, n, PANEL):
        columns = [jnp.broadcast_to(work[:, k : k + 1], (n, 2 * n)) for k in range(start, start + PANEL)]
        rows = [work[k : k + 1, :] for k in range(start, start + PANEL)]
        update = jnp.zeros((n, 2 * n), jnp.float32)
        for i in range(PANEL):
            k = start + i
            scale = lax.rsqrt(columns[i][k : k + 1, :])
            column = columns[i] * scale
            pivot_row = rows[i] * scale
            for later in range(i + 1, PANEL):
                weight = column[start + later : start + later + 1, :]
                columns[later] = columns[later] - column * weight
                rows[later] = rows[later] - pivot_row * weight
            update = update + jnp.where(row > k, column, 0.0) * pivot_row
            lower = jnp.where((lane == k) & (row >= k), column, lower)
            scales = jnp.where(row == k, scale, scales)
        work = work - update
    inverse = (work * scales)[:, n:]
    return lower[:, :n], inverse


def kernel(
    steps, group_count, owner_count,
    start_ref, shift_ref, rows_ref, cols_ref, live_ref, tiles_hbm,
    proj_ref, fac_ref, next_ref,
    tiles_ref, turned, masks, products, gathered, stage, history, own, own_history, back_out, back_in, direct_out, direct_in,
    pair_out, pair_in, dots_grp, basis, images, transform, place_vector, place_ref, tile_sem, place_sem,
    gather_send, gather_recv, relay_send, relay_recv, own_send, own_recv,
    pair_send, pair_recv, back_send, back_recv, direct_send, direct_recv, dots_send, dots_recv,
):
    g = lax.axis_index("grp")
    r = lax.axis_index("row")
    width = start_ref.shape[0]
    row_count = start_ref.shape[1]
    part = row_count // group_count
    tile_count = tiles_ref.shape[0]
    owned = row_count // tiles_ref.shape[1]
    chips = owner_count // 2
    chip, core = r // 2, lax.rem(r, 2)
    partner = chip * 2 + 1 - core
    chip_x, chip_z = lax.rem(chip, SIDE), chip // SIDE

    def away(d):
        return min(d % SIDE, SIDE - d % SIDE) + min(d // SIDE, chips // SIDE - d // SIDE)

    offsets = sorted(range(1, chips), key=lambda d: -away(d))

    def chip_at(d, sign):
        z_count = chips // SIDE
        return lax.rem(chip_z + (sign * (d // SIDE)) % z_count, z_count) * SIDE + lax.rem(
            chip_x + (sign * (d % SIDE)) % SIDE, SIDE
        )

    sources = [chip_at(d, -1) for d in offsets]
    targets = [chip_at(d, 1) for d in offsets]
    grp_peers = [lax.rem(g + d, group_count) for d in range(1, group_count)]
    total_cols = steps * width

    barrier = pltpu.get_barrier_semaphore()
    for peer in targets:
        pl.semaphore_signal(barrier, inc=1, device_id=(g, peer * 2 + core), device_id_type=MESH)
    pl.semaphore_signal(barrier, inc=1, device_id=(g, partner), device_id_type=MESH)
    for peer in grp_peers:
        pl.semaphore_signal(barrier, inc=1, device_id=(peer, r), device_id_type=MESH)
    load = pltpu.make_async_copy(tiles_hbm, tiles_ref, tile_sem)
    load.start()

    def to_row(peer, src, dst, send, recv):
        return pltpu.make_async_remote_copy(
            src_ref=src, dst_ref=dst, send_sem=send, recv_sem=recv,
            device_id=(g, peer), device_id_type=MESH,
        )

    def to_grp(peer, src, dst, send, recv):
        return pltpu.make_async_remote_copy(
            src_ref=src, dst_ref=dst, send_sem=send, recv_sem=recv,
            device_id=(peer, r), device_id_type=MESH,
        )

    others = group_count - 1

    def send_vectors(half, operand):
        gathered[half, r] = operand
        own[g] = operand
        for peer in grp_peers:
            to_grp(peer, own.at[g], own.at[g], own_send, own_recv).start()
        for i, peer in enumerate(targets):
            to_row(
                peer * 2 + core, gathered.at[half, r], gathered.at[half, r], gather_send, gather_recv.at[i]
            ).start()
        to_row(partner, gathered.at[half, r], gathered.at[half, r], gather_send, relay_recv.at[half]).start()
        stage[r] = operand

    def sent_vectors():
        bulk = gathered.at[0, pl.ds(0, chips)]
        to_row(partner, bulk, bulk, gather_send, gather_send).wait_send()
        bulk = own.at[pl.ds(0, others)]
        to_grp(grp_peers[0], bulk, bulk, own_send, own_send).wait_send()

    def take_own():
        bulk = own.at[pl.ds(0, others)]
        to_grp(grp_peers[0], bulk, bulk, own_recv, own_recv).wait_recv()

    def keep_own(step):
        for i in range(group_count):
            own_history[step * width : (step + 1) * width, i * part : (i + 1) * part] = own[i]

    def relay_vectors(half):
        for i, peer in reversed(list(enumerate(sources))):
            slot = peer * 2 + core
            block = gathered.at[half, slot]
            to_row(slot, block, block, gather_send, gather_recv.at[i]).wait_recv()
            to_row(partner, block, block, relay_send, relay_recv.at[half]).start()
            stage[slot] = gathered[half, slot]

    def relays_sent():
        bulk = gathered.at[0, pl.ds(0, chips - 1)]
        to_row(partner, bulk, bulk, relay_send, relay_send).wait_send()

    def take_relayed(half):
        bulk = gathered.at[half, pl.ds(0, chips)]
        to_row(partner, bulk, bulk, gather_send, relay_recv.at[half]).wait_recv()
        for peer in range(chips):
            slot = peer * 2 + 1 - core
            stage[slot] = gathered[half, slot]

    fold = 128 // width

    def pack(square):
        height = width // fold
        return jnp.concatenate([square[i * height : (i + 1) * height] for i in range(fold)], axis=1)

    def unpack(packed):
        return jnp.concatenate([packed[:, i * width : (i + 1) * width] for i in range(fold)], axis=0)

    def part_dots(step, parity):
        dots = jnp.zeros(((step + 1) * width, width), jnp.float32)
        for peer in range(chips):
            slot = peer * 2 + parity
            vector = stage[slot]
            left = vector
            if step > 0:
                left = jnp.concatenate([history[slot, : step * width, :], vector], axis=0)
            dots = dots + lax.dot_general(left, vector, NT, preferred_element_type=jnp.float32)
        return dots

    def send_dots(step, half, dots):
        height = width // fold
        dots_grp[half, g, :height] = pack(dots[step * width :])
        if step > 0:
            old = dots[: step * width]
            if step < steps:
                old = jnp.concatenate([old, jnp.zeros((total_cols - step * width, width), jnp.float32)], axis=0)
            dots_grp[half, g, height:] = old.T
        rows = height if step == 0 else height + width
        for peer in grp_peers:
            to_grp(
                peer, dots_grp.at[half, g, pl.ds(0, rows)], dots_grp.at[half, g, pl.ds(0, rows)],
                dots_send, dots_recv.at[half],
            ).start()

    def dots_bulk(step, half):
        height = width // fold
        return dots_grp.at[half, pl.ds(0, others), pl.ds(0, height if step == 0 else height + width)]

    def take_dots(step, half):
        height = width // fold
        bulk = dots_bulk(step, half)
        to_grp(grp_peers[0], bulk, bulk, dots_send, dots_recv.at[half]).wait_recv()
        rows = height if step == 0 else height + width
        summed = dots_grp[half, 0, :rows]
        for index in range(1, group_count):
            summed = summed + dots_grp[half, index, :rows]
        gram = unpack(summed[:height])
        if step == 0:
            return None, gram
        cross = dot_nt(summed[height:], transform[...])
        return cross, gram - dot_nt(cross, cross)

    def dots_sent(step, half):
        bulk = dots_bulk(step, half)
        to_grp(grp_peers[0], bulk, bulk, dots_send, dots_recv.at[half]).wait_send()

    def back_product(slot):
        value = products[place_ref[0, slot]]
        for i in range(1, owned):
            value = value + products[place_ref[0, i * owner_count + slot]]
        return value

    def take_pair(peer, half):
        return pair_in[half, peer].astype(jnp.float32)

    mine = pl.ds(pl.multiple_of(g * part, part), part)
    current = start_ref[:, mine]
    shift = shift_ref[:, mine]
    pl.semaphore_wait(barrier, chips + others)
    send_vectors(0, current.astype(jnp.bfloat16))
    lanes = lax.broadcasted_iota(jnp.int32, place_vector.shape, 1)
    place = jnp.full(place_vector.shape, tile_count, jnp.int32)
    for k in range(tile_count):
        alive = k < live_ref[0]
        position = jnp.where(alive, rows_ref[k] * owner_count + cols_ref[k], -1)
        place = jnp.where(lanes == position, k, place)
        row = jnp.full((16, 128), jnp.where(alive, rows_ref[k], -1), jnp.int32)
        for i in range(owned):
            masks[k, i] = jnp.where(row == i, 1.0, 0.0).astype(jnp.bfloat16)
    place_vector[...] = place
    place_copy = pltpu.make_async_copy(place_vector, place_ref, place_sem)
    place_copy.start()
    basis[...] = jnp.zeros_like(basis)
    images[...] = jnp.zeros_like(images)
    transform[...] = jnp.zeros_like(transform)
    products[tile_count] = jnp.zeros((width, part), jnp.float32)
    load.wait()

    def turn(j, carry):
        for i in range(4):
            turned[j * 4 + i] = tiles_ref[j * 4 + i].T
        return carry

    lax.fori_loop(0, tile_count // 4, turn, 0)
    place_copy.wait()

    coef = None
    lane = lax.broadcasted_iota(jnp.int32, (width, total_cols), 1)
    sub = lax.broadcasted_iota(jnp.int32, (width, total_cols), 0)
    for step in range(steps):
        half = step % 2
        take_own()
        for k in range(tile_count):
            products[k] = jnp.dot(own[rows_ref[k]], tiles_ref[k], preferred_element_type=jnp.float32)
        for i, peer in enumerate(targets + [chip]):
            pair_out[peer] = back_product(peer * 2 + 1 - core).astype(jnp.bfloat16)
            to_row(partner, pair_out.at[peer], pair_in.at[half, peer], pair_send, pair_recv.at[half]).start()
        keep_own(step)
        relay_vectors(half)
        dots = part_dots(step, core)
        to_row(partner, pair_out, pair_in.at[half], pair_send, pair_recv.at[half]).wait_recv()
        for peer in targets:
            back_out[peer] = (back_product(peer * 2 + core) + take_pair(peer, half)).astype(jnp.bfloat16)
            to_row(peer * 2 + core, back_out.at[peer], back_in.at[half, chip], back_send, back_recv.at[half]).start()
        total = back_product(r) + take_pair(chip, half)
        take_relayed(half)
        send_dots(step, half, dots + part_dots(step, 1 - core))
        forward = jnp.zeros((owned * width, part), jnp.float32)
        for k in range(tile_count):
            vector = stage[cols_ref[k]]
            spread = []
            for i in range(owned):
                mask = masks[k, i]
                mask = jnp.concatenate([jnp.concatenate([mask, mask], axis=1)] * (width // 16), axis=0)
                spread.append(vector * mask)
            forward = forward + jnp.dot(
                jnp.concatenate(spread, axis=0), turned[k], preferred_element_type=jnp.float32
            )
        for i in range(owned):
            direct_out[i] = forward[i * width : (i + 1) * width].astype(jnp.bfloat16)
        for peer in grp_peers:
            to_grp(peer, direct_out.at[peer], direct_in.at[g], direct_send, direct_recv).start()
        for i in range(owned):
            total = total + forward[i * width : (i + 1) * width] * jnp.where(g == i, 1.0, 0.0)
        for slot in range(owner_count):
            history[slot, step * width : (step + 1) * width, :] = stage[slot]
        sent_vectors()
        relays_sent()
        cross, gram = take_dots(step, half)
        left, rest = current, None
        if step > 0:
            left = left - dot_nn(cross, basis[...])
            rest = dot_nn(cross, images[...])
        lower, inverse = factor_and_inverse(gram)
        now = dot_nn(inverse, left)
        ahead = now * (MIDDLE - shift)
        if step > 0:
            follow = lower.T
            ahead = ahead - dot_nn(follow, basis[(step - 1) * width : step * width, :])
        bulk = back_in.at[half, pl.ds(0, chips - 1)]
        to_row(partner, bulk, bulk, back_send, back_recv.at[half]).wait_recv()
        for peer in sources:
            total = total + back_in[half, peer].astype(jnp.float32)
        bulk = direct_in.at[pl.ds(0, others)]
        to_grp(grp_peers[0], bulk, bulk, direct_send, direct_recv).wait_recv()
        for peer in grp_peers:
            total = total + direct_in[peer].astype(jnp.float32)
        total = 0.5 * total
        if step > 0:
            total = total - rest
        image = dot_nn(inverse, total)
        current = image + ahead
        send_vectors(1 - half, current.astype(jnp.bfloat16))
        basis[step * width : (step + 1) * width, :] = now
        images[step * width : (step + 1) * width, :] = image
        if step > 0:
            proj_ref[step - 1] = cross + coef
            fac_ref[step - 1] = lower
        unit = jnp.where(lane == step * width + sub, 1.0, 0.0)
        if step == 0:
            transform[:width, :] = dot_nn(inverse, unit)
            coef = -MIDDLE * unit
        else:
            transform[step * width : (step + 1) * width, :] = dot_nn(inverse, unit - dot_nn(cross, transform[...]))
            wide = jnp.concatenate([follow] * (total_cols // width), axis=1)
            coef = -MIDDLE * unit + jnp.where((lane >= (step - 1) * width) & (lane < step * width), wide, 0.0)
        to_row(partner, pair_out, pair_out, pair_send, pair_recv.at[half]).wait_send()
        bulk = back_out.at[pl.ds(0, chips - 1)]
        to_row(partner, bulk, bulk, back_send, back_recv.at[half]).wait_send()
        bulk = direct_out.at[pl.ds(0, others)]
        to_grp(grp_peers[0], bulk, bulk, direct_send, direct_recv).wait_send()
        dots_sent(step, half)

    half = steps % 2
    take_own()
    keep_own(steps)
    relay_vectors(half)
    dots = part_dots(steps, core)
    take_relayed(half)
    send_dots(steps, half, dots + part_dots(steps, 1 - core))
    sent_vectors()
    relays_sent()
    cross, gram = take_dots(steps, half)
    lower, inverse = factor_and_inverse(gram)
    proj_ref[steps - 1] = cross + coef
    fac_ref[steps - 1] = lower
    combine = jnp.concatenate([-dot_nn(inverse, dot_nn(cross, transform[...])), inverse], axis=1)
    high = combine.astype(jnp.bfloat16)
    low = (combine - high.astype(jnp.float32)).astype(jnp.bfloat16)
    both = jnp.dot(jnp.concatenate([high, low], axis=0), own_history[...], preferred_element_type=jnp.float32)
    next_ref[...] = both[:width] + both[width:]
    dots_sent(steps, half)


def hand_on(proj_in, fac_in, next_in, proj_ref, fac_ref, next_ref):
    proj_ref[...] = proj_in[...]
    fac_ref[...] = fac_in[...]
    next_ref[...] = next_in[...]


def per_device(tiles, tile_rows, tile_cols, live_tiles, dual_shift, start_block):
    matrix = tiles[0, 0]
    tile_count, edge = matrix.shape[0], matrix.shape[1]
    width, row_count = start_block.shape
    group_count = lax.axis_size("grp")
    owner_count = lax.axis_size("row")
    owned = row_count // edge
    part = row_count // group_count
    total_cols = ITERS * width
    vmem = pl.BlockSpec(memory_space=pltpu.VMEM)
    smem = pl.BlockSpec(memory_space=pltpu.SMEM)
    dma = pltpu.SemaphoreType.DMA
    packed = width + width * width // 128
    shapes = (
            jax.ShapeDtypeStruct((ITERS, width, total_cols), jnp.float32),
            jax.ShapeDtypeStruct((ITERS, width, width), jnp.float32),
            jax.ShapeDtypeStruct((width, row_count), jnp.float32),
    )
    outs = pl.pallas_call(
        functools.partial(kernel, ITERS, group_count, owner_count),
        out_shape=shapes,
        in_specs=[vmem, vmem, smem, smem, smem, pl.BlockSpec(memory_space=pltpu.HBM)],
        out_specs=(vmem, vmem, vmem),
        scratch_shapes=[
            pltpu.VMEM(matrix.shape, jnp.bfloat16),
            pltpu.VMEM(matrix.shape, jnp.bfloat16),
            pltpu.VMEM((tile_count, owned, 16, 128), jnp.bfloat16),
            pltpu.VMEM((tile_count + 1, width, part), jnp.float32),
            pltpu.VMEM((2, owner_count, width, part), jnp.bfloat16),
            pltpu.VMEM((owner_count, width, part), jnp.bfloat16),
            pltpu.VMEM((owner_count, total_cols, part), jnp.bfloat16),
            pltpu.VMEM((group_count, width, part), jnp.bfloat16),
            pltpu.VMEM((total_cols + width, row_count), jnp.bfloat16),
            pltpu.VMEM((owner_count // 2, width, part), jnp.bfloat16),
            pltpu.VMEM((2, owner_count // 2, width, part), jnp.bfloat16),
            pltpu.VMEM((group_count, width, part), jnp.bfloat16),
            pltpu.VMEM((group_count, width, part), jnp.bfloat16),
            pltpu.VMEM((owner_count // 2, width, part), jnp.bfloat16),
            pltpu.VMEM((2, owner_count // 2, width, part), jnp.bfloat16),
            pltpu.VMEM((2, group_count, packed, total_cols), jnp.float32),
            pltpu.VMEM((total_cols, part), jnp.float32),
            pltpu.VMEM((total_cols, part), jnp.float32),
            pltpu.VMEM((total_cols, total_cols), jnp.float32),
            pltpu.VMEM((8, owned * owner_count), jnp.int32),
            pltpu.SMEM((8, owned * owner_count), jnp.int32),
            dma, dma,
            dma, dma((owner_count // 2 - 1,)), dma, dma((2,)), dma, dma,
            dma, dma((2,)), dma, dma((2,)), dma, dma, dma, dma((2,)),
        ],
        compiler_params=pltpu.CompilerParams(
            collective_id=0, has_side_effects=True, vmem_limit_bytes=60 * 1024 * 1024
        ),
    )(start_block, dual_shift[None, :], tile_rows[0, 0], tile_cols[0, 0], live_tiles[0], matrix)
    return pl.pallas_call(hand_on, out_shape=shapes, in_specs=[vmem] * 3, out_specs=(vmem,) * 3)(*outs)


def solution(mesh):
    in_specs = (
        P("grp", "row", None, None, None),
        P("grp", "row", None),
        P("grp", "row", None),
        P("grp", "row"),
        P("row"),
        P(None, "row"),
    )
    out_specs = (P(), P(), P(None, "row"))
    return jax.shard_map(
        per_device, mesh=mesh, in_specs=in_specs, out_specs=out_specs, check_vma=False
    )
```

time: 95.1 us -> 78 us (0.82)
  Pallas kernels: 86.5 us -> 76.5 us
  local copies, waits for them, and re-layouts: 6.96 us -> 0 us
    pallas_call x1, Pallas kernels: 84.9 us -> 74.9 us  [per_device(): pl.pallas_call(functools.partial(kernel, ITERS, group_count, owner_count)...]
    unnamed x16 -> x0, local copies, waits for them, and re-layouts: 6.96 us -> none
where the time goes in v3:
time: 78 us; the launch traced here: 77.8 us
  Pallas kernels  76.5 us (98%)
  between operations  1.29 us (2%)
    pallas_call x1, Pallas kernels, per_device(): pl.pallas_call(functools.partial(kernel, ITERS, group_count, owner_count)...  74.9 us
    pallas_call x1, Pallas kernels, per_device(): pl.pallas_call(hand_on, out_shape=shapes, in_specs=[vmem] * 3, out_specs=...  1.68 us

profile of v3, /device:TPU:1, one launch (start us, length us, event | category | flops | bytes accessed | tf_op | source)
XLA Modules:
  0.0 77.8 jit_solution(8071571173706216765)
XLA Ops:
  1.3 74.9 %shard_map.85 = (f32[4,32,128]{2,1,0:T(8,128)}, f32[4,32,32]{2,1,0:T(8,128)}, f32[32,1024]{1,0:T(8,128)}) custom-call(f32[32,1024]{1,0:T(8,128)} %start_ref.1, f32[1,1024]{1,0:T(1,128)} %bitcast.7, s32[32]{0:T(128)} %bitcast.8, s32[32]{0:T(128)} %bitcast.9, s32[1]{0:T(128)} %bitcast.5.live_ref, bf16[32,256,256]{2,1,0:T(8,128)(2,1)} %bitcast.6), custom_call_target="tpu_custom_call" | custom-call | tf_op jit(solution)/shard_map/pallas_call | solution.py:389
  76.2 1.7 %shard_map.86 = (f32[4,32,128]{2,1,0:T(8,128)}, f32[4,32,32]{2,1,0:T(8,128)}, f32[32,1024]{1,0:T(8,128)}) custom-call(f32[4,32,128]{2,1,0:T(8,128)} %get-tuple-element.6.proj_in, f32[4,32,32]{2,1,0:T(8,128)} %get-tuple-element.7.fac_in, f32[32,1024]{1,0:T(8,128)} %get-tuple-element.8.next_in), custom_call_target="tpu_custom_call" | custom-call | tf_op jit(solution)/shard_map/pallas_call | solution.py:424

commit v4 on v3

--- a/solution.py
+++ b/solution.py
@@ -57,9 +57,9 @@
     start_ref, shift_ref, rows_ref, cols_ref, live_ref, tiles_hbm,
     proj_ref, fac_ref, next_ref,
     tiles_ref, turned, masks, products, gathered, stage, history, own, own_history, back_out, back_in, direct_out, direct_in,
-    pair_out, pair_in, dots_grp, basis, images, transform, place_vector, place_ref, tile_sem, place_sem,
+    pair_out, pair_in, dots_pair, dots_grp, basis, images, transform, place_vector, place_ref, tile_sem, place_sem,
     gather_send, gather_recv, relay_send, relay_recv, own_send, own_recv,
-    pair_send, pair_recv, back_send, back_recv, direct_send, direct_recv, dots_send, dots_recv,
+    pair_send, pair_recv, back_send, back_recv, direct_send, direct_recv, dots_send, dots_recv, dpair_send, dpair_recv,
 ):
     g = lax.axis_index("grp")
     r = lax.axis_index("row")
@@ -86,7 +86,8 @@
 
     sources = [chip_at(d, -1) for d in offsets]
     targets = [chip_at(d, 1) for d in offsets]
-    grp_peers = [lax.rem(g + d, group_count) for d in range(1, group_count)]
+    grp_order = sorted(range(1, group_count), key=lambda d: -min(d, group_count - d))
+    grp_peers = [lax.rem(g + d, group_count) for d in grp_order]
     total_cols = steps * width
 
     barrier = pltpu.get_barrier_semaphore()
@@ -112,7 +113,7 @@
 
     others = group_count - 1
 
-    def send_vectors(half, operand):
+    def send_vectors(half, operand, relayed=True):
         gathered[half, r] = operand
         own[g] = operand
         for peer in grp_peers:
@@ -121,11 +122,12 @@
             to_row(
                 peer * 2 + core, gathered.at[half, r], gathered.at[half, r], gather_send, gather_recv.at[i]
             ).start()
-        to_row(partner, gathered.at[half, r], gathered.at[half, r], gather_send, relay_recv.at[half]).start()
+        if relayed:
+            to_row(partner, gathered.at[half, r], gathered.at[half, r], gather_send, relay_recv.at[half]).start()
         stage[r] = operand
 
-    def sent_vectors():
-        bulk = gathered.at[0, pl.ds(0, chips)]
+    def sent_vectors(relayed=True):
+        bulk = gathered.at[0, pl.ds(0, chips if relayed else chips - 1)]
         to_row(partner, bulk, bulk, gather_send, gather_send).wait_send()
         bulk = own.at[pl.ds(0, others)]
         to_grp(grp_peers[0], bulk, bulk, own_send, own_send).wait_send()
@@ -157,61 +159,75 @@
             slot = peer * 2 + 1 - core
             stage[slot] = gathered[half, slot]
 
-    fold = 128 // width
-
-    def pack(square):
-        height = width // fold
-        return jnp.concatenate([square[i * height : (i + 1) * height] for i in range(fold)], axis=1)
-
-    def unpack(packed):
-        return jnp.concatenate([packed[:, i * width : (i + 1) * width] for i in range(fold)], axis=0)
-
-    def part_dots(step, parity):
-        dots = jnp.zeros(((step + 1) * width, width), jnp.float32)
+    def pack(dots):
+        pieces, done, count = [], 0, dots.shape[1]
+        for size in (128, 64, 32):
+            while count - done >= size:
+                height = width * size // 128
+                piece = dots[:, done : done + size]
+                pieces.append(
+                    jnp.concatenate([piece[i * height : (i + 1) * height] for i in range(width // height)], axis=1)
+                )
+                done += size
+        return jnp.concatenate(pieces, axis=0)
+
+    def unpack(packed, count):
+        pieces, done, row = [], 0, 0
+        for size in (128, 64, 32):
+            while count - done >= size:
+                height = width * size // 128
+                piece = packed[row : row + height]
+                pieces.append(
+                    jnp.concatenate([piece[:, i * size : (i + 1) * size] for i in range(width // height)], axis=0)
+                )
+                done += size
+                row += height
+        return pieces
+
+    def packed_rows(step):
+        return pl.ds(0, (step + 1) * width * width // 128)
+
+    def send_pair_dots(step, half):
+        dots = jnp.zeros((width, (step + 1) * width), jnp.float32)
         for peer in range(chips):
-            slot = peer * 2 + parity
+            slot = peer * 2 + core
             vector = stage[slot]
-            left = vector
+            right = vector
             if step > 0:
-                left = jnp.concatenate([history[slot, : step * width, :], vector], axis=0)
-            dots = dots + lax.dot_general(left, vector, NT, preferred_element_type=jnp.float32)
-        return dots
-
-    def send_dots(step, half, dots):
-        height = width // fold
-        dots_grp[half, g, :height] = pack(dots[step * width :])
-        if step > 0:
-            old = dots[: step * width]
-            if step < steps:
-                old = jnp.concatenate([old, jnp.zeros((total_cols - step * width, width), jnp.float32)], axis=0)
-            dots_grp[half, g, height:] = old.T
-        rows = height if step == 0 else height + width
+                right = jnp.concatenate([vector, history[slot, : step * width, :]], axis=0)
+            dots = dots + lax.dot_general(vector, right, NT, preferred_element_type=jnp.float32)
+        rows = packed_rows(step)
+        dots_pair[half, core, rows] = pack(dots)
+        mine = dots_pair.at[half, core, rows]
+        to_row(partner, mine, mine, dpair_send, dpair_recv.at[half]).start()
+
+    def send_dots(step, half):
+        rows = packed_rows(step)
+        block = dots_pair.at[half, 0, rows]
+        to_row(partner, block, block, dpair_send, dpair_recv.at[half]).wait()
+        dots_grp[half, g, rows] = dots_pair[half, 0, rows] + dots_pair[half, 1, rows]
         for peer in grp_peers:
             to_grp(
-                peer, dots_grp.at[half, g, pl.ds(0, rows)], dots_grp.at[half, g, pl.ds(0, rows)],
-                dots_send, dots_recv.at[half],
+                peer, dots_grp.at[half, g, rows], dots_grp.at[half, g, rows], dots_send, dots_recv.at[half]
             ).start()
 
-    def dots_bulk(step, half):
-        height = width // fold
-        return dots_grp.at[half, pl.ds(0, others), pl.ds(0, height if step == 0 else height + width)]
-
     def take_dots(step, half):
-        height = width // fold
-        bulk = dots_bulk(step, half)
+        rows = packed_rows(step)
+        bulk = dots_grp.at[half, pl.ds(0, others), rows]
         to_grp(grp_peers[0], bulk, bulk, dots_send, dots_recv.at[half]).wait_recv()
-        rows = height if step == 0 else height + width
-        summed = dots_grp[half, 0, :rows]
+        summed = dots_grp[half, 0, rows]
         for index in range(1, group_count):
-            summed = summed + dots_grp[half, index, :rows]
-        gram = unpack(summed[:height])
+            summed = summed + dots_grp[half, index, rows]
+        pieces = unpack(summed, (step + 1) * width)
+        gram = pieces[0][:, :width]
         if step == 0:
             return None, gram
-        cross = dot_nt(summed[height:], transform[...])
+        whole = jnp.concatenate(pieces, axis=1) if len(pieces) > 1 else pieces[0]
+        cross = dot_nt(whole[:, width:], transform[:, : step * width])
         return cross, gram - dot_nt(cross, cross)
 
     def dots_sent(step, half):
-        bulk = dots_bulk(step, half)
+        bulk = dots_grp.at[half, pl.ds(0, others), packed_rows(step)]
         to_grp(grp_peers[0], bulk, bulk, dots_send, dots_recv.at[half]).wait_send()
 
     def back_product(slot):
@@ -267,14 +283,14 @@
             to_row(partner, pair_out.at[peer], pair_in.at[half, peer], pair_send, pair_recv.at[half]).start()
         keep_own(step)
         relay_vectors(half)
-        dots = part_dots(step, core)
+        send_pair_dots(step, half)
         to_row(partner, pair_out, pair_in.at[half], pair_send, pair_recv.at[half]).wait_recv()
         for peer in targets:
             back_out[peer] = (back_product(peer * 2 + core) + take_pair(peer, half)).astype(jnp.bfloat16)
             to_row(peer * 2 + core, back_out.at[peer], back_in.at[half, chip], back_send, back_recv.at[half]).start()
         total = back_product(r) + take_pair(chip, half)
+        send_dots(step, half)
         take_relayed(half)
-        send_dots(step, half, dots + part_dots(step, 1 - core))
         forward = jnp.zeros((owned * width, part), jnp.float32)
         for k in range(tile_count):
             vector = stage[cols_ref[k]]
@@ -302,11 +318,6 @@
             left = left - dot_nn(cross, basis[...])
             rest = dot_nn(cross, images[...])
         lower, inverse = factor_and_inverse(gram)
-        now = dot_nn(inverse, left)
-        ahead = now * (MIDDLE - shift)
-        if step > 0:
-            follow = lower.T
-            ahead = ahead - dot_nn(follow, basis[(step - 1) * width : step * width, :])
         bulk = back_in.at[half, pl.ds(0, chips - 1)]
         to_row(partner, bulk, bulk, back_send, back_recv.at[half]).wait_recv()
         for peer in sources:
@@ -318,9 +329,14 @@
         total = 0.5 * total
         if step > 0:
             total = total - rest
+        now = dot_nn(inverse, left)
+        ahead = now * (MIDDLE - shift)
+        if step > 0:
+            follow = lower.T
+            ahead = ahead - dot_nn(follow, basis[(step - 1) * width : step * width, :])
         image = dot_nn(inverse, total)
         current = image + ahead
-        send_vectors(1 - half, current.astype(jnp.bfloat16))
+        send_vectors(1 - half, current.astype(jnp.bfloat16), step < steps - 1)
         basis[step * width : (step + 1) * width, :] = now
         images[step * width : (step + 1) * width, :] = image
         if step > 0:
@@ -342,14 +358,16 @@
         dots_sent(step, half)
 
     half = steps % 2
+    for i, peer in reversed(list(enumerate(sources))):
+        slot = peer * 2 + core
+        block = gathered.at[half, slot]
+        to_row(slot, block, block, gather_send, gather_recv.at[i]).wait_recv()
+        stage[slot] = gathered[half, slot]
+    send_pair_dots(steps, half)
     take_own()
     keep_own(steps)
-    relay_vectors(half)
-    dots = part_dots(steps, core)
-    take_relayed(half)
-    send_dots(steps, half, dots + part_dots(steps, 1 - core))
-    sent_vectors()
-    relays_sent()
+    sent_vectors(False)
+    send_dots(steps, half)
     cross, gram = take_dots(steps, half)
     lower, inverse = factor_and_inverse(gram)
     proj_ref[steps - 1] = cross + coef
@@ -407,6 +425,7 @@
             pltpu.VMEM((group_count, width, part), jnp.bfloat16),
             pltpu.VMEM((owner_count // 2, width, part), jnp.bfloat16),
             pltpu.VMEM((2, owner_count // 2, width, part), jnp.bfloat16),
+            pltpu.VMEM((2, 2, packed, total_cols), jnp.float32),
             pltpu.VMEM((2, group_count, packed, total_cols), jnp.float32),
             pltpu.VMEM((total_cols, part), jnp.float32),
             pltpu.VMEM((total_cols, part), jnp.float32),
@@ -415,7 +434,7 @@
             pltpu.SMEM((8, owned * owner_count), jnp.int32),
             dma, dma,
             dma, dma((owner_count // 2 - 1,)), dma, dma((2,)), dma, dma,
-            dma, dma((2,)), dma, dma((2,)), dma, dma, dma, dma((2,)),
+            dma, dma((2,)), dma, dma((2,)), dma, dma, dma, dma((2,)), dma, dma((2,)),
         ],
         compiler_params=pltpu.CompilerParams(
             collective_id=0, has_side_effects=True, vmem_limit_bytes=60 * 1024 * 1024

time: 78 us -> 75.2 us (0.964)
  Pallas kernels: 76.5 us -> 73.8 us
    pallas_call x1, Pallas kernels: 74.9 us -> 72.1 us  [per_device(): pl.pallas_call(functools.partial(kernel, ITERS, group_count, owner_count)...]
where the time goes in v4:
time: 75.2 us; the launch traced here: 75 us
  Pallas kernels  73.8 us (98%)
  between operations  1.29 us (2%)
    pallas_call x1, Pallas kernels, per_device(): pl.pallas_call(functools.partial(kernel, ITERS, group_count, owner_count)...  72.1 us
    pallas_call x1, Pallas kernels, per_device(): pl.pallas_call(hand_on, out_shape=shapes, in_specs=[vmem] * 3, out_specs=...  1.68 us

profile of v4, /device:TPU:1, one launch (start us, length us, event | category | flops | bytes accessed | tf_op | source)
XLA Modules:
  0.0 75.0 jit_solution(8891943554867392046)
XLA Ops:
  1.3 72.1 %shard_map.85 = (f32[4,32,128]{2,1,0:T(8,128)}, f32[4,32,32]{2,1,0:T(8,128)}, f32[32,1024]{1,0:T(8,128)}) custom-call(f32[32,1024]{1,0:T(8,128)} %start_ref.1, f32[1,1024]{1,0:T(1,128)} %bitcast.7, s32[32]{0:T(128)} %bitcast.8, s32[32]{0:T(128)} %bitcast.9, s32[1]{0:T(128)} %bitcast.5.live_ref, bf16[32,256,256]{2,1,0:T(8,128)(2,1)} %bitcast.6), custom_call_target="tpu_custom_call" | custom-call | tf_op jit(solution)/shard_map/pallas_call | solution.py:407
  73.4 1.7 %shard_map.86 = (f32[4,32,128]{2,1,0:T(8,128)}, f32[4,32,32]{2,1,0:T(8,128)}, f32[32,1024]{1,0:T(8,128)}) custom-call(f32[4,32,128]{2,1,0:T(8,128)} %get-tuple-element.6.proj_in, f32[4,32,32]{2,1,0:T(8,128)} %get-tuple-element.7.fac_in, f32[32,1024]{1,0:T(8,128)} %get-tuple-element.8.next_in), custom_call_target="tpu_custom_call" | custom-call | tf_op jit(solution)/shard_map/pallas_call | solution.py:443

commit v5 on v4

--- a/solution.py
+++ b/solution.py
@@ -26,37 +26,38 @@
 
 def factor_and_inverse(gram):
     n = gram.shape[0]
-    row = lax.broadcasted_iota(jnp.int32, (n, 2 * n), 0)
-    lane = lax.broadcasted_iota(jnp.int32, (n, 2 * n), 1)
-    work = jnp.concatenate([gram, jnp.where(row == lane, 1.0, 0.0)[:, :n]], axis=1)
-    lower = jnp.zeros((n, 2 * n), jnp.float32)
-    scales = jnp.zeros((n, 2 * n), jnp.float32)
+    row = lax.broadcasted_iota(jnp.int32, (n, n), 0)
+    lane = lax.broadcasted_iota(jnp.int32, (n, n), 1)
+    within = lax.broadcasted_iota(jnp.int32, (PANEL, 2 * n), 0)
+    work = jnp.concatenate([gram, jnp.where(row == lane, 1.0, 0.0)], axis=1)
+    blocks = []
     for start in range(0, n, PANEL):
-        columns = [jnp.broadcast_to(work[:, k : k + 1], (n, 2 * n)) for k in range(start, start + PANEL)]
-        rows = [work[k : k + 1, :] for k in range(start, start + PANEL)]
-        update = jnp.zeros((n, 2 * n), jnp.float32)
+        columns = [jnp.broadcast_to(work[:, k : k + 1], work.shape) for k in range(start, start + PANEL)]
+        rows = [work[i : i + 1, :] for i in range(PANEL)]
+        block = jnp.zeros((PANEL, 2 * n), jnp.float32)
         for i in range(PANEL):
-            k = start + i
-            scale = lax.rsqrt(columns[i][k : k + 1, :])
-            column = columns[i] * scale
-            pivot_row = rows[i] * scale
+            scale = lax.rsqrt(columns[i][i : i + 1, :])
+            columns[i] = columns[i] * scale
+            rows[i] = rows[i] * scale
             for later in range(i + 1, PANEL):
-                weight = column[start + later : start + later + 1, :]
-                columns[later] = columns[later] - column * weight
-                rows[later] = rows[later] - pivot_row * weight
-            update = update + jnp.where(row > k, column, 0.0) * pivot_row
-            lower = jnp.where((lane == k) & (row >= k), column, lower)
-            scales = jnp.where(row == k, scale, scales)
-        work = work - update
-    inverse = (work * scales)[:, n:]
-    return lower[:, :n], inverse
+                weight = columns[i][later : later + 1, :]
+                columns[later] = columns[later] - columns[i] * weight
+                rows[later] = rows[later] - rows[i] * weight
+            block = jnp.where(within == i, rows[i], block)
+        blocks.append(block)
+        work = work[PANEL:]
+        if start + PANEL < n:
+            for i in range(PANEL):
+                work = work - columns[i][PANEL:] * rows[i]
+    whole = jnp.concatenate(blocks, axis=0)
+    return jnp.where(lane >= row, whole[:, :n], 0.0), whole[:, n:]
 
 
 def kernel(
     steps, group_count, owner_count,
-    start_ref, shift_ref, rows_ref, cols_ref, live_ref, tiles_hbm,
+    start_hbm, shift_hbm, rows_hbm, cols_hbm, live_ref, tiles_hbm,
     proj_ref, fac_ref, next_ref,
-    tiles_ref, turned, masks, products, gathered, stage, history, own, own_history, back_out, back_in, direct_out, direct_in,
+    start_ref, shift_ref, rows_ref, cols_ref, input_sem, tiles_ref, turned, masks, products, gathered, stage, history, own, own_history, back_out, back_in, direct_out, direct_in,
     pair_out, pair_in, dots_pair, dots_grp, basis, images, transform, place_vector, place_ref, tile_sem, place_sem,
     gather_send, gather_recv, relay_send, relay_recv, own_send, own_recv,
     pair_send, pair_recv, back_send, back_recv, direct_send, direct_recv, dots_send, dots_recv, dpair_send, dpair_recv,
@@ -96,6 +97,14 @@
     pl.semaphore_signal(barrier, inc=1, device_id=(g, partner), device_id_type=MESH)
     for peer in grp_peers:
         pl.semaphore_signal(barrier, inc=1, device_id=(peer, r), device_id_type=MESH)
+    inputs = [
+        pltpu.make_async_copy(src, dst, input_sem.at[i])
+        for i, (src, dst) in enumerate(
+            [(start_hbm, start_ref), (shift_hbm, shift_ref), (rows_hbm, rows_ref), (cols_hbm, cols_ref)]
+        )
+    ]
+    for copy in inputs:
+        copy.start()
     load = pltpu.make_async_copy(tiles_hbm, tiles_ref, tile_sem)
     load.start()
 
@@ -113,11 +122,12 @@
 
     others = group_count - 1
 
-    def send_vectors(half, operand, relayed=True):
+    def send_vectors(half, operand, relayed=True, own_too=True):
         gathered[half, r] = operand
-        own[g] = operand
-        for peer in grp_peers:
-            to_grp(peer, own.at[g], own.at[g], own_send, own_recv).start()
+        if own_too:
+            own[g] = operand
+            for peer in grp_peers:
+                to_grp(peer, own.at[g], own.at[g], own_send, own_recv).start()
         for i, peer in enumerate(targets):
             to_row(
                 peer * 2 + core, gathered.at[half, r], gathered.at[half, r], gather_send, gather_recv.at[i]
@@ -126,11 +136,12 @@
             to_row(partner, gathered.at[half, r], gathered.at[half, r], gather_send, relay_recv.at[half]).start()
         stage[r] = operand
 
-    def sent_vectors(relayed=True):
+    def sent_vectors(relayed=True, own_too=True):
         bulk = gathered.at[0, pl.ds(0, chips if relayed else chips - 1)]
         to_row(partner, bulk, bulk, gather_send, gather_send).wait_send()
-        bulk = own.at[pl.ds(0, others)]
-        to_grp(grp_peers[0], bulk, bulk, own_send, own_send).wait_send()
+        if own_too:
+            bulk = own.at[pl.ds(0, others)]
+            to_grp(grp_peers[0], bulk, bulk, own_send, own_send).wait_send()
 
     def take_own():
         bulk = own.at[pl.ds(0, others)]
@@ -140,13 +151,21 @@
         for i in range(group_count):
             own_history[step * width : (step + 1) * width, i * part : (i + 1) * part] = own[i]
 
-    def relay_vectors(half):
-        for i, peer in reversed(list(enumerate(sources))):
+    def take_gathered(step, half):
+        dots, batch = None, [r]
+        for count, (i, peer) in enumerate(reversed(list(enumerate(sources)))):
             slot = peer * 2 + core
             block = gathered.at[half, slot]
             to_row(slot, block, block, gather_send, gather_recv.at[i]).wait_recv()
-            to_row(partner, block, block, relay_send, relay_recv.at[half]).start()
+            if step < steps:
+                to_row(partner, block, block, relay_send, relay_recv.at[half]).start()
             stage[slot] = gathered[half, slot]
+            batch.append(slot)
+            if count % 5 == 4:
+                value = slot_dots(step, batch)
+                dots = value if dots is None else dots + value
+                batch = []
+        return dots
 
     def relays_sent():
         bulk = gathered.at[0, pl.ds(0, chips - 1)]
@@ -187,15 +206,17 @@
     def packed_rows(step):
         return pl.ds(0, (step + 1) * width * width // 128)
 
-    def send_pair_dots(step, half):
+    def slot_dots(step, slots):
         dots = jnp.zeros((width, (step + 1) * width), jnp.float32)
-        for peer in range(chips):
-            slot = peer * 2 + core
+        for slot in slots:
             vector = stage[slot]
             right = vector
             if step > 0:
                 right = jnp.concatenate([vector, history[slot, : step * width, :]], axis=0)
             dots = dots + lax.dot_general(vector, right, NT, preferred_element_type=jnp.float32)
+        return dots
+
+    def send_pair_dots(step, half, dots):
         rows = packed_rows(step)
         dots_pair[half, core, rows] = pack(dots)
         mine = dots_pair.at[half, core, rows]
@@ -240,10 +261,14 @@
         return pair_in[half, peer].astype(jnp.float32)
 
     mine = pl.ds(pl.multiple_of(g * part, part), part)
+    for copy in inputs:
+        copy.wait()
     current = start_ref[:, mine]
     shift = shift_ref[:, mine]
     pl.semaphore_wait(barrier, chips + others)
-    send_vectors(0, current.astype(jnp.bfloat16))
+    send_vectors(0, current.astype(jnp.bfloat16), own_too=False)
+    for i in range(group_count):
+        own[i] = start_ref[:, i * part : (i + 1) * part].astype(jnp.bfloat16)
     lanes = lax.broadcasted_iota(jnp.int32, place_vector.shape, 1)
     place = jnp.full(place_vector.shape, tile_count, jnp.int32)
     for k in range(tile_count):
@@ -261,29 +286,30 @@
     transform[...] = jnp.zeros_like(transform)
     products[tile_count] = jnp.zeros((width, part), jnp.float32)
     load.wait()
+    place_copy.wait()
 
     def turn(j, carry):
         for i in range(4):
             turned[j * 4 + i] = tiles_ref[j * 4 + i].T
         return carry
-
-    lax.fori_loop(0, tile_count // 4, turn, 0)
-    place_copy.wait()
 
     coef = None
     lane = lax.broadcasted_iota(jnp.int32, (width, total_cols), 1)
     sub = lax.broadcasted_iota(jnp.int32, (width, total_cols), 0)
     for step in range(steps):
         half = step % 2
-        take_own()
+        if step > 0:
+            take_own()
         for k in range(tile_count):
             products[k] = jnp.dot(own[rows_ref[k]], tiles_ref[k], preferred_element_type=jnp.float32)
         for i, peer in enumerate(targets + [chip]):
             pair_out[peer] = back_product(peer * 2 + 1 - core).astype(jnp.bfloat16)
             to_row(partner, pair_out.at[peer], pair_in.at[half, peer], pair_send, pair_recv.at[half]).start()
         keep_own(step)
-        relay_vectors(half)
-        send_pair_dots(step, half)
+        if step == 0:
+            lax.fori_loop(0, tile_count // 4, turn, 0)
+        dots = take_gathered(step, half)
+        send_pair_dots(step, half, dots)
         to_row(partner, pair_out, pair_in.at[half], pair_send, pair_recv.at[half]).wait_recv()
         for peer in targets:
             back_out[peer] = (back_product(peer * 2 + core) + take_pair(peer, half)).astype(jnp.bfloat16)
@@ -310,14 +336,18 @@
             total = total + forward[i * width : (i + 1) * width] * jnp.where(g == i, 1.0, 0.0)
         for slot in range(owner_count):
             history[slot, step * width : (step + 1) * width, :] = stage[slot]
-        sent_vectors()
+        sent_vectors(own_too=step > 0)
         relays_sent()
         cross, gram = take_dots(step, half)
         left, rest = current, None
         if step > 0:
             left = left - dot_nn(cross, basis[...])
             rest = dot_nn(cross, images[...])
-        lower, inverse = factor_and_inverse(gram)
+        upper, inverse = factor_and_inverse(gram)
+        now = dot_nn(inverse, left)
+        ahead = now * (MIDDLE - shift)
+        if step > 0:
+            ahead = ahead - dot_nn(upper, basis[(step - 1) * width : step * width, :])
         bulk = back_in.at[half, pl.ds(0, chips - 1)]
         to_row(partner, bulk, bulk, back_send, back_recv.at[half]).wait_recv()
         for peer in sources:
@@ -329,11 +359,6 @@
         total = 0.5 * total
         if step > 0:
             total = total - rest
-        now = dot_nn(inverse, left)
-        ahead = now * (MIDDLE - shift)
-        if step > 0:
-            follow = lower.T
-            ahead = ahead - dot_nn(follow, basis[(step - 1) * width : step * width, :])
         image = dot_nn(inverse, total)
         current = image + ahead
         send_vectors(1 - half, current.astype(jnp.bfloat16), step < steps - 1)
@@ -341,14 +366,14 @@
         images[step * width : (step + 1) * width, :] = image
         if step > 0:
             proj_ref[step - 1] = cross + coef
-            fac_ref[step - 1] = lower
+            fac_ref[step - 1] = upper.T
         unit = jnp.where(lane == step * width + sub, 1.0, 0.0)
         if step == 0:
             transform[:width, :] = dot_nn(inverse, unit)
             coef = -MIDDLE * unit
         else:
             transform[step * width : (step + 1) * width, :] = dot_nn(inverse, unit - dot_nn(cross, transform[...]))
-            wide = jnp.concatenate([follow] * (total_cols // width), axis=1)
+            wide = jnp.concatenate([upper] * (total_cols // width), axis=1)
             coef = -MIDDLE * unit + jnp.where((lane >= (step - 1) * width) & (lane < step * width), wide, 0.0)
         to_row(partner, pair_out, pair_out, pair_send, pair_recv.at[half]).wait_send()
         bulk = back_out.at[pl.ds(0, chips - 1)]
@@ -358,20 +383,16 @@
         dots_sent(step, half)
 
     half = steps % 2
-    for i, peer in reversed(list(enumerate(sources))):
-        slot = peer * 2 + core
-        block = gathered.at[half, slot]
-        to_row(slot, block, block, gather_send, gather_recv.at[i]).wait_recv()
-        stage[slot] = gathered[half, slot]
-    send_pair_dots(steps, half)
+    dots = take_gathered(steps, half)
+    send_pair_dots(steps, half, dots)
     take_own()
     keep_own(steps)
     sent_vectors(False)
     send_dots(steps, half)
     cross, gram = take_dots(steps, half)
-    lower, inverse = factor_and_inverse(gram)
+    upper, inverse = factor_and_inverse(gram)
     proj_ref[steps - 1] = cross + coef
-    fac_ref[steps - 1] = lower
+    fac_ref[steps - 1] = upper.T
     combine = jnp.concatenate([-dot_nn(inverse, dot_nn(cross, transform[...])), inverse], axis=1)
     high = combine.astype(jnp.bfloat16)
     low = (combine - high.astype(jnp.float32)).astype(jnp.bfloat16)
@@ -397,6 +418,7 @@
     total_cols = ITERS * width
     vmem = pl.BlockSpec(memory_space=pltpu.VMEM)
     smem = pl.BlockSpec(memory_space=pltpu.SMEM)
+    hbm = pl.BlockSpec(memory_space=pltpu.HBM)
     dma = pltpu.SemaphoreType.DMA
     packed = width + width * width // 128
     shapes = (
@@ -406,10 +428,15 @@
     )
     outs = pl.pallas_call(
         functools.partial(kernel, ITERS, group_count, owner_count),
-        out_shape=shapes,
-        in_specs=[vmem, vmem, smem, smem, smem, pl.BlockSpec(memory_space=pltpu.HBM)],
+        out_shape=tuple(pltpu.VMEM(x.shape, x.dtype) for x in shapes),
+        in_specs=[hbm, hbm, hbm, hbm, smem, hbm],
         out_specs=(vmem, vmem, vmem),
         scratch_shapes=[
+            pltpu.VMEM((width, row_count), jnp.float32),
+            pltpu.VMEM((1, row_count), jnp.float32),
+            pltpu.SMEM((tile_count,), jnp.int32),
+            pltpu.SMEM((tile_count,), jnp.int32),
+            dma((4,)),
             pltpu.VMEM(matrix.shape, jnp.bfloat16),
             pltpu.VMEM(matrix.shape, jnp.bfloat16),
             pltpu.VMEM((tile_count, owned, 16, 128), jnp.bfloat16),
@@ -440,7 +467,8 @@
             collective_id=0, has_side_effects=True, vmem_limit_bytes=60 * 1024 * 1024
         ),
     )(start_block, dual_shift[None, :], tile_rows[0, 0], tile_cols[0, 0], live_tiles[0], matrix)
-    return pl.pallas_call(hand_on, out_shape=shapes, in_specs=[vmem] * 3, out_specs=(vmem,) * 3)(*outs)
+    return pl.pallas_call(hand_on, out_shape=shapes, in_specs=[vmem] * 3, out_specs=(vmem,) * 3,
+        compiler_params=pltpu.CompilerParams(vmem_limit_bytes=2 * 1024 * 1024))(*outs)
 
 
 def solution(mesh):

time: 75.2 us -> 71.8 us (0.955)
  Pallas kernels: 73.8 us -> 70.3 us
    pallas_call x1, Pallas kernels: 72.1 us -> 69.6 us  [per_device(): pl.pallas_call(functools.partial(kernel, ITERS, group_count, owner_count)...]
    pallas_call x1, Pallas kernels: 1.68 us -> 0.72 us  [per_device(): pl.pallas_call(hand_on, out_shape=shapes, in_specs=[vmem] * 3, out_specs=...]
where the time goes in v5:
time: 71.8 us; the launch traced here: 71.6 us
  Pallas kernels  70.3 us (98%)
  between operations  1.29 us (2%)
    pallas_call x1, Pallas kernels, per_device(): pl.pallas_call(functools.partial(kernel, ITERS, group_count, owner_count)...  69.6 us

profile of v5, /device:TPU:1, one launch (start us, length us, event | category | flops | bytes accessed | tf_op | source)
XLA Modules:
  0.0 71.6 jit_solution(11912709824377586942)
XLA Ops:
  1.3 69.6 %shard_map.85 = (f32[4,32,128]{2,1,0:T(8,128)S(1)}, f32[4,32,32]{2,1,0:T(8,128)S(1)}, f32[32,1024]{1,0:T(8,128)S(1)}) custom-call(f32[32,1024]{1,0:T(8,128)} %start_hbm.1, f32[1,1024]{1,0:T(1,128)} %bitcast.7, s32[32]{0:T(128)} %bitcast.8, s32[32]{0:T(128)} %bitcast.9, s32[1]{0:T(128)} %bitcast.5.live_ref, bf16[32,256,256]{2,1,0:T(8,128)(2,1)} %bitcast.6), custom_call_target="tpu_custom_call" | custom-call | tf_op jit(solution)/shard_map/pallas_call | solution.py:429
  70.9 0.7 %shard_map.86 = (f32[4,32,128]{2,1,0:T(8,128)}, f32[4,32,32]{2,1,0:T(8,128)}, f32[32,1024]{1,0:T(8,128)}) custom-call(f32[4,32,128]{2,1,0:T(8,128)S(1)} %get-tuple-element.6.proj_in, f32[4,32,32]{2,1,0:T(8,128)S(1)} %get-tuple-element.7.fac_in, f32[32,1024]{1,0:T(8,128)S(1)} %get-tuple-element.8.next_in), custom_call_target="tpu_custom_call" | custom-call | tf_op jit(solution)/shard_map/pallas_call | solution.py:470

commit v6 on v5

--- a/solution.py
+++ b/solution.py
@@ -12,8 +12,9 @@
 HIGH = lax.Precision.HIGHEST
 NT = (((1,), (1,)), ((), ()))
 MIDDLE = 1.25
-PANEL = 8
+PANEL = 16
 SIDE = 4
+NEAR = 2
 
 
 def dot_nt(a, b):
@@ -53,14 +54,22 @@
     return jnp.where(lane >= row, whole[:, :n], 0.0), whole[:, n:]
 
 
+def away(d, chips):
+    return min(d % SIDE, SIDE - d % SIDE) + min(d // SIDE, chips // SIDE - d // SIDE)
+
+
+def far_first(chips):
+    return sorted(range(1, chips), key=lambda d: -away(d, chips))
+
+
 def kernel(
     steps, group_count, owner_count,
     start_hbm, shift_hbm, rows_hbm, cols_hbm, live_ref, tiles_hbm,
     proj_ref, fac_ref, next_ref,
     start_ref, shift_ref, rows_ref, cols_ref, input_sem, tiles_ref, turned, masks, products, gathered, stage, history, own, own_history, back_out, back_in, direct_out, direct_in,
-    pair_out, pair_in, dots_pair, dots_grp, basis, images, transform, place_vector, place_ref, tile_sem, place_sem,
+    pair_out, pair_in, dots_grp, basis, images, transform, place_vector, place_ref, tile_sem, place_sem,
     gather_send, gather_recv, relay_send, relay_recv, own_send, own_recv,
-    pair_send, pair_recv, back_send, back_recv, direct_send, direct_recv, dots_send, dots_recv, dpair_send, dpair_recv,
+    pair_send, pair_recv, back_send, back_recv, direct_send, direct_recv, dots_send, dots_recv,
 ):
     g = lax.axis_index("grp")
     r = lax.axis_index("row")
@@ -74,10 +83,7 @@
     partner = chip * 2 + 1 - core
     chip_x, chip_z = lax.rem(chip, SIDE), chip // SIDE
 
-    def away(d):
-        return min(d % SIDE, SIDE - d % SIDE) + min(d // SIDE, chips // SIDE - d // SIDE)
-
-    offsets = sorted(range(1, chips), key=lambda d: -away(d))
+    offsets = far_first(chips)
 
     def chip_at(d, sign):
         z_count = chips // SIDE
@@ -85,6 +91,7 @@
             chip_x + (sign * (d % SIDE)) % SIDE, SIDE
         )
 
+    far_count = sum(away(d, chips) > NEAR for d in offsets)
     sources = [chip_at(d, -1) for d in offsets]
     targets = [chip_at(d, 1) for d in offsets]
     grp_order = sorted(range(1, group_count), key=lambda d: -min(d, group_count - d))
@@ -94,9 +101,12 @@
     barrier = pltpu.get_barrier_semaphore()
     for peer in targets:
         pl.semaphore_signal(barrier, inc=1, device_id=(g, peer * 2 + core), device_id_type=MESH)
+    for peer in targets[:far_count]:
+        pl.semaphore_signal(barrier, inc=1, device_id=(g, peer * 2 + 1 - core), device_id_type=MESH)
     pl.semaphore_signal(barrier, inc=1, device_id=(g, partner), device_id_type=MESH)
     for peer in grp_peers:
         pl.semaphore_signal(barrier, inc=1, device_id=(peer, r), device_id_type=MESH)
+        pl.semaphore_signal(barrier, inc=1, device_id=(peer, partner), device_id_type=MESH)
     inputs = [
         pltpu.make_async_copy(src, dst, input_sem.at[i])
         for i, (src, dst) in enumerate(
@@ -130,7 +140,7 @@
                 to_grp(peer, own.at[g], own.at[g], own_send, own_recv).start()
         for i, peer in enumerate(targets):
             to_row(
-                peer * 2 + core, gathered.at[half, r], gathered.at[half, r], gather_send, gather_recv.at[i]
+                peer * 2 + core, gathered.at[half, r], gathered.at[half, r], gather_send, gather_recv.at[half, i]
             ).start()
         if relayed:
             to_row(partner, gathered.at[half, r], gathered.at[half, r], gather_send, relay_recv.at[half]).start()
@@ -156,7 +166,7 @@
         for count, (i, peer) in enumerate(reversed(list(enumerate(sources)))):
             slot = peer * 2 + core
             block = gathered.at[half, slot]
-            to_row(slot, block, block, gather_send, gather_recv.at[i]).wait_recv()
+            to_row(slot, block, block, gather_send, gather_recv.at[half, i]).wait_recv()
             if step < steps:
                 to_row(partner, block, block, relay_send, relay_recv.at[half]).start()
             stage[slot] = gathered[half, slot]
@@ -204,7 +214,7 @@
         return pieces
 
     def packed_rows(step):
-        return pl.ds(0, (step + 1) * width * width // 128)
+        return pl.ds(0, 16 + (step + 1) // 2 * 16)
 
     def slot_dots(step, slots):
         dots = jnp.zeros((width, (step + 1) * width), jnp.float32)
@@ -216,39 +226,43 @@
             dots = dots + lax.dot_general(vector, right, NT, preferred_element_type=jnp.float32)
         return dots
 
-    def send_pair_dots(step, half, dots):
+    def send_dots(step, half, dots):
         rows = packed_rows(step)
-        dots_pair[half, core, rows] = pack(dots)
-        mine = dots_pair.at[half, core, rows]
-        to_row(partner, mine, mine, dpair_send, dpair_recv.at[half]).start()
-
-    def send_dots(step, half):
-        rows = packed_rows(step)
-        block = dots_pair.at[half, 0, rows]
-        to_row(partner, block, block, dpair_send, dpair_recv.at[half]).wait()
-        dots_grp[half, g, rows] = dots_pair[half, 0, rows] + dots_pair[half, 1, rows]
+        me = g * 2 + core
+        gram = pack(dots[:, :width])
+        high = gram.astype(jnp.bfloat16).astype(jnp.float32)
+        dots_grp[half, me, :16] = jnp.concatenate([high, gram - high], axis=0).astype(jnp.bfloat16)
+        if step > 0:
+            cross = pack(dots[:, width:])
+            if step % 2 == 1:
+                cross = jnp.concatenate([cross, jnp.zeros((8, 128), jnp.float32)], axis=0)
+            dots_grp[half, me, 16 : 16 + cross.shape[0]] = cross.astype(jnp.bfloat16)
+        block = dots_grp.at[half, me, rows]
         for peer in grp_peers:
-            to_grp(
-                peer, dots_grp.at[half, g, rows], dots_grp.at[half, g, rows], dots_send, dots_recv.at[half]
+            to_grp(peer, block, block, dots_send, dots_recv.at[half]).start()
+            pltpu.make_async_remote_copy(
+                src_ref=block, dst_ref=block, send_sem=dots_send, recv_sem=dots_recv.at[half],
+                device_id=(peer, partner), device_id_type=MESH,
             ).start()
+        to_row(partner, block, block, dots_send, dots_recv.at[half]).start()
 
     def take_dots(step, half):
         rows = packed_rows(step)
-        bulk = dots_grp.at[half, pl.ds(0, others), rows]
+        bulk = dots_grp.at[half, pl.ds(0, 2 * group_count - 1), rows]
         to_grp(grp_peers[0], bulk, bulk, dots_send, dots_recv.at[half]).wait_recv()
-        summed = dots_grp[half, 0, rows]
-        for index in range(1, group_count):
-            summed = summed + dots_grp[half, index, rows]
-        pieces = unpack(summed, (step + 1) * width)
-        gram = pieces[0][:, :width]
+        summed = dots_grp[half, 0, rows].astype(jnp.float32)
+        for index in range(1, 2 * group_count):
+            summed = summed + dots_grp[half, index, rows].astype(jnp.float32)
+        gram = unpack(summed[:8] + summed[8:16], width)[0]
         if step == 0:
             return None, gram
+        pieces = unpack(summed[16:], step * width)
         whole = jnp.concatenate(pieces, axis=1) if len(pieces) > 1 else pieces[0]
-        cross = dot_nt(whole[:, width:], transform[:, : step * width])
+        cross = dot_nt(whole, transform[:, : step * width])
         return cross, gram - dot_nt(cross, cross)
 
     def dots_sent(step, half):
-        bulk = dots_grp.at[half, pl.ds(0, others), packed_rows(step)]
+        bulk = dots_grp.at[half, pl.ds(0, 2 * group_count - 1), packed_rows(step)]
         to_grp(grp_peers[0], bulk, bulk, dots_send, dots_recv.at[half]).wait_send()
 
     def back_product(slot):
@@ -265,7 +279,7 @@
         copy.wait()
     current = start_ref[:, mine]
     shift = shift_ref[:, mine]
-    pl.semaphore_wait(barrier, chips + others)
+    pl.semaphore_wait(barrier, chips + far_count + 2 * others)
     send_vectors(0, current.astype(jnp.bfloat16), own_too=False)
     for i in range(group_count):
         own[i] = start_ref[:, i * part : (i + 1) * part].astype(jnp.bfloat16)
@@ -298,24 +312,44 @@
     sub = lax.broadcasted_iota(jnp.int32, (width, total_cols), 0)
     for step in range(steps):
         half = step % 2
+        far = far_count if step > 0 else 0
+        near_rows = pl.ds(0, chips - far)
         if step > 0:
             take_own()
         for k in range(tile_count):
             products[k] = jnp.dot(own[rows_ref[k]], tiles_ref[k], preferred_element_type=jnp.float32)
-        for i, peer in enumerate(targets + [chip]):
-            pair_out[peer] = back_product(peer * 2 + 1 - core).astype(jnp.bfloat16)
-            to_row(partner, pair_out.at[peer], pair_in.at[half, peer], pair_send, pair_recv.at[half]).start()
+        for i, peer in enumerate(targets[far:] + [chip]):
+            pair_out[i] = back_product(peer * 2 + 1 - core).astype(jnp.bfloat16)
+            to_row(partner, pair_out.at[i], pair_in.at[half, i], pair_send, pair_recv.at[half]).start()
+        for i, peer in enumerate(targets[:far]):
+            for side, slot in enumerate([peer * 2 + core, peer * 2 + 1 - core]):
+                index = 2 * i + side
+                back_out[index] = back_product(slot).astype(jnp.bfloat16)
+                to_row(
+                    slot, back_out.at[index], back_in.at[half, index], back_send, back_recv.at[half]
+                ).start()
         keep_own(step)
         if step == 0:
             lax.fori_loop(0, tile_count // 4, turn, 0)
+        def send_back():
+            to_row(
+                partner, pair_out.at[near_rows], pair_in.at[half, near_rows], pair_send, pair_recv.at[half]
+            ).wait_recv()
+            for i, peer in enumerate(targets[far:]):
+                index = 2 * far + i
+                back_out[index] = (back_product(peer * 2 + core) + take_pair(i, half)).astype(jnp.bfloat16)
+                to_row(
+                    peer * 2 + core, back_out.at[index], back_in.at[half, index], back_send, back_recv.at[half]
+                ).start()
+            total = back_product(r) + take_pair(len(targets) - far, half)
+            return total
+
+        if step == 0:
+            total = send_back()
         dots = take_gathered(step, half)
-        send_pair_dots(step, half, dots)
-        to_row(partner, pair_out, pair_in.at[half], pair_send, pair_recv.at[half]).wait_recv()
-        for peer in targets:
-            back_out[peer] = (back_product(peer * 2 + core) + take_pair(peer, half)).astype(jnp.bfloat16)
-            to_row(peer * 2 + core, back_out.at[peer], back_in.at[half, chip], back_send, back_recv.at[half]).start()
-        total = back_product(r) + take_pair(chip, half)
-        send_dots(step, half)
+        send_dots(step, half, dots)
+        if step > 0:
+            total = send_back()
         take_relayed(half)
         forward = jnp.zeros((owned * width, part), jnp.float32)
         for k in range(tile_count):
@@ -348,10 +382,10 @@
         ahead = now * (MIDDLE - shift)
         if step > 0:
             ahead = ahead - dot_nn(upper, basis[(step - 1) * width : step * width, :])
-        bulk = back_in.at[half, pl.ds(0, chips - 1)]
+        bulk = back_in.at[half, pl.ds(0, chips - 1 + far)]
         to_row(partner, bulk, bulk, back_send, back_recv.at[half]).wait_recv()
-        for peer in sources:
-            total = total + back_in[half, peer].astype(jnp.float32)
+        for index in range(chips - 1 + far):
+            total = total + back_in[half, index].astype(jnp.float32)
         bulk = direct_in.at[pl.ds(0, others)]
         to_grp(grp_peers[0], bulk, bulk, direct_send, direct_recv).wait_recv()
         for peer in grp_peers:
@@ -375,8 +409,9 @@
             transform[step * width : (step + 1) * width, :] = dot_nn(inverse, unit - dot_nn(cross, transform[...]))
             wide = jnp.concatenate([upper] * (total_cols // width), axis=1)
             coef = -MIDDLE * unit + jnp.where((lane >= (step - 1) * width) & (lane < step * width), wide, 0.0)
-        to_row(partner, pair_out, pair_out, pair_send, pair_recv.at[half]).wait_send()
-        bulk = back_out.at[pl.ds(0, chips - 1)]
+        bulk = pair_out.at[near_rows]
+        to_row(partner, bulk, bulk, pair_send, pair_recv.at[half]).wait_send()
+        bulk = back_out.at[pl.ds(0, chips - 1 + far)]
         to_row(partner, bulk, bulk, back_send, back_recv.at[half]).wait_send()
         bulk = direct_out.at[pl.ds(0, others)]
         to_grp(grp_peers[0], bulk, bulk, direct_send, direct_recv).wait_send()
@@ -384,20 +419,22 @@
 
     half = steps % 2
     dots = take_gathered(steps, half)
-    send_pair_dots(steps, half, dots)
+    send_dots(steps, half, dots)
     take_own()
     keep_own(steps)
     sent_vectors(False)
-    send_dots(steps, half)
     cross, gram = take_dots(steps, half)
+    combine = dot_nn(cross, transform[...])
+    high = combine.astype(jnp.bfloat16)
+    low = (combine - high.astype(jnp.float32)).astype(jnp.bfloat16)
+    both = jnp.dot(
+        jnp.concatenate([high, low], axis=0), own_history[:total_cols, :], preferred_element_type=jnp.float32
+    )
+    left = own_history[total_cols:, :].astype(jnp.float32) - both[:width] - both[width:]
     upper, inverse = factor_and_inverse(gram)
     proj_ref[steps - 1] = cross + coef
     fac_ref[steps - 1] = upper.T
-    combine = jnp.concatenate([-dot_nn(inverse, dot_nn(cross, transform[...])), inverse], axis=1)
-    high = combine.astype(jnp.bfloat16)
-    low = (combine - high.astype(jnp.float32)).astype(jnp.bfloat16)
-    both = jnp.dot(jnp.concatenate([high, low], axis=0), own_history[...], preferred_element_type=jnp.float32)
-    next_ref[...] = both[:width] + both[width:]
+    next_ref[...] = dot_nn(inverse, left)
     dots_sent(steps, half)
 
 
@@ -420,7 +457,11 @@
     smem = pl.BlockSpec(memory_space=pltpu.SMEM)
     hbm = pl.BlockSpec(memory_space=pltpu.HBM)
     dma = pltpu.SemaphoreType.DMA
-    packed = width + width * width // 128
+    chips = owner_count // 2
+    far = sum(away(d, chips) > NEAR for d in far_first(chips))
+    back_count = chips - 1 + far
+    pair_count = chips
+    packed = 16 + (ITERS + 1) // 2 * 16
     shapes = (
             jax.ShapeDtypeStruct((ITERS, width, total_cols), jnp.float32),
             jax.ShapeDtypeStruct((ITERS, width, width), jnp.float32),
@@ -446,22 +487,21 @@
             pltpu.VMEM((owner_count, total_cols, part), jnp.bfloat16),
             pltpu.VMEM((group_count, width, part), jnp.bfloat16),
             pltpu.VMEM((total_cols + width, row_count), jnp.bfloat16),
-            pltpu.VMEM((owner_count // 2, width, part), jnp.bfloat16),
-            pltpu.VMEM((2, owner_count // 2, width, part), jnp.bfloat16),
+            pltpu.VMEM((back_count, width, part), jnp.bfloat16),
+            pltpu.VMEM((2, back_count, width, part), jnp.bfloat16),
             pltpu.VMEM((group_count, width, part), jnp.bfloat16),
             pltpu.VMEM((group_count, width, part), jnp.bfloat16),
-            pltpu.VMEM((owner_count // 2, width, part), jnp.bfloat16),
-            pltpu.VMEM((2, owner_count // 2, width, part), jnp.bfloat16),
-            pltpu.VMEM((2, 2, packed, total_cols), jnp.float32),
-            pltpu.VMEM((2, group_count, packed, total_cols), jnp.float32),
+            pltpu.VMEM((pair_count, width, part), jnp.bfloat16),
+            pltpu.VMEM((2, pair_count, width, part), jnp.bfloat16),
+            pltpu.VMEM((2, 2 * group_count, packed, total_cols), jnp.bfloat16),
             pltpu.VMEM((total_cols, part), jnp.float32),
             pltpu.VMEM((total_cols, part), jnp.float32),
             pltpu.VMEM((total_cols, total_cols), jnp.float32),
             pltpu.VMEM((8, owned * owner_count), jnp.int32),
             pltpu.SMEM((8, owned * owner_count), jnp.int32),
             dma, dma,
-            dma, dma((owner_count // 2 - 1,)), dma, dma((2,)), dma, dma,
-            dma, dma((2,)), dma, dma((2,)), dma, dma, dma, dma((2,)), dma, dma((2,)),
+            dma, dma((2, owner_count // 2 - 1)), dma, dma((2,)), dma, dma,
+            dma, dma((2,)), dma, dma((2,)), dma, dma, dma, dma((2,)),
         ],
         compiler_params=pltpu.CompilerParams(
             collective_id=0, has_side_effects=True, vmem_limit_bytes=60 * 1024 * 1024

time: 71.8 us -> 70.6 us (0.983)
  Pallas kernels: 70.3 us -> 69.2 us
    pallas_call x1, Pallas kernels: 69.6 us -> 68.5 us  [per_device(): pl.pallas_call(functools.partial(kernel, ITERS, group_count, owner_count)...]
where the time goes in v6:
time: 70.6 us; the launch traced here: 70.5 us
  Pallas kernels  69.2 us (98%)
  between operations  1.29 us (2%)
    pallas_call x1, Pallas kernels, per_device(): pl.pallas_call(functools.partial(kernel, ITERS, group_count, owner_count)...  68.5 us

profile of v6, /device:TPU:1, one launch (start us, length us, event | category | flops | bytes accessed | tf_op | source)
XLA Modules:
  0.0 70.5 jit_solution(13515779666347767514)
XLA Ops:
  1.3 68.5 %shard_map.85 = (f32[4,32,128]{2,1,0:T(8,128)S(1)}, f32[4,32,32]{2,1,0:T(8,128)S(1)}, f32[32,1024]{1,0:T(8,128)S(1)}) custom-call(f32[32,1024]{1,0:T(8,128)} %start_hbm.1, f32[1,1024]{1,0:T(1,128)} %bitcast.7, s32[32]{0:T(128)} %bitcast.8, s32[32]{0:T(128)} %bitcast.9, s32[1]{0:T(128)} %bitcast.5.live_ref, bf16[32,256,256]{2,1,0:T(8,128)(2,1)} %bitcast.6), custom_call_target="tpu_custom_call" | custom-call | tf_op jit(solution)/shard_map/pallas_call | solution.py:470
  69.8 0.7 %shard_map.86 = (f32[4,32,128]{2,1,0:T(8,128)}, f32[4,32,32]{2,1,0:T(8,128)}, f32[32,1024]{1,0:T(8,128)}) custom-call(f32[4,32,128]{2,1,0:T(8,128)S(1)} %get-tuple-element.6.proj_in, f32[4,32,32]{2,1,0:T(8,128)S(1)} %get-tuple-element.7.fac_in, f32[32,1024]{1,0:T(8,128)S(1)} %get-tuple-element.8.next_in), custom_call_target="tpu_custom_call" | custom-call | tf_op jit(solution)/shard_map/pallas_call | solution.py:510

commit v7 on v6

--- a/solution.py
+++ b/solution.py
@@ -36,15 +36,24 @@
         columns = [jnp.broadcast_to(work[:, k : k + 1], work.shape) for k in range(start, start + PANEL)]
         rows = [work[i : i + 1, :] for i in range(PANEL)]
         block = jnp.zeros((PANEL, 2 * n), jnp.float32)
-        for i in range(PANEL):
-            scale = lax.rsqrt(columns[i][i : i + 1, :])
-            columns[i] = columns[i] * scale
-            rows[i] = rows[i] * scale
-            for later in range(i + 1, PANEL):
-                weight = columns[i][later : later + 1, :]
-                columns[later] = columns[later] - columns[i] * weight
-                rows[later] = rows[later] - rows[i] * weight
+        for i in range(0, PANEL, 2):
+            first, second = columns[i], columns[i + 1]
+            corner, cross, other = first[i : i + 1, :], first[i + 1 : i + 2, :], second[i + 1 : i + 2, :]
+            det = corner * other - cross * cross
+            scale, root = lax.rsqrt(corner), lax.rsqrt(det)
+            left, right = root * scale * corner, root * scale * cross
+            columns[i] = first * scale
+            columns[i + 1] = second * left - first * right
+            upper_row, lower_row = rows[i], rows[i + 1]
+            rows[i] = upper_row * scale
+            rows[i + 1] = lower_row * left - upper_row * right
+            for later in range(i + 2, PANEL):
+                for k in (i, i + 1):
+                    weight = columns[k][later : later + 1, :]
+                    columns[later] = columns[later] - columns[k] * weight
+                    rows[later] = rows[later] - rows[k] * weight
             block = jnp.where(within == i, rows[i], block)
+            block = jnp.where(within == i + 1, rows[i + 1], block)
         blocks.append(block)
         work = work[PANEL:]
         if start + PANEL < n:
@@ -98,15 +107,6 @@
     grp_peers = [lax.rem(g + d, group_count) for d in grp_order]
     total_cols = steps * width
 
-    barrier = pltpu.get_barrier_semaphore()
-    for peer in targets:
-        pl.semaphore_signal(barrier, inc=1, device_id=(g, peer * 2 + core), device_id_type=MESH)
-    for peer in targets[:far_count]:
-        pl.semaphore_signal(barrier, inc=1, device_id=(g, peer * 2 + 1 - core), device_id_type=MESH)
-    pl.semaphore_signal(barrier, inc=1, device_id=(g, partner), device_id_type=MESH)
-    for peer in grp_peers:
-        pl.semaphore_signal(barrier, inc=1, device_id=(peer, r), device_id_type=MESH)
-        pl.semaphore_signal(barrier, inc=1, device_id=(peer, partner), device_id_type=MESH)
     inputs = [
         pltpu.make_async_copy(src, dst, input_sem.at[i])
         for i, (src, dst) in enumerate(
@@ -117,6 +117,12 @@
         copy.start()
     load = pltpu.make_async_copy(tiles_hbm, tiles_ref, tile_sem)
     load.start()
+    barrier = pltpu.get_barrier_semaphore()
+    for peer in targets:
+        pl.semaphore_signal(barrier, inc=1, device_id=(g, peer * 2 + core), device_id_type=MESH)
+    pl.semaphore_signal(barrier, inc=1, device_id=(g, partner), device_id_type=MESH)
+    for peer in grp_peers:
+        pl.semaphore_signal(barrier, inc=1, device_id=(peer, r), device_id_type=MESH)
 
     def to_row(peer, src, dst, send, recv):
         return pltpu.make_async_remote_copy(
@@ -279,7 +285,7 @@
         copy.wait()
     current = start_ref[:, mine]
     shift = shift_ref[:, mine]
-    pl.semaphore_wait(barrier, chips + far_count + 2 * others)
+    pl.semaphore_wait(barrier, chips + others)
     send_vectors(0, current.astype(jnp.bfloat16), own_too=False)
     for i in range(group_count):
         own[i] = start_ref[:, i * part : (i + 1) * part].astype(jnp.bfloat16)
@@ -289,9 +295,9 @@
         alive = k < live_ref[0]
         position = jnp.where(alive, rows_ref[k] * owner_count + cols_ref[k], -1)
         place = jnp.where(lanes == position, k, place)
-        row = jnp.full((16, 128), jnp.where(alive, rows_ref[k], -1), jnp.int32)
+        row = jnp.full((8, 128), jnp.where(alive, rows_ref[k], -1), jnp.int32)
         for i in range(owned):
-            masks[k, i] = jnp.where(row == i, 1.0, 0.0).astype(jnp.bfloat16)
+            masks[k, i] = jnp.where(row == i, 1.0, 0.0)
     place_vector[...] = place
     place_copy = pltpu.make_async_copy(place_vector, place_ref, place_sem)
     place_copy.start()
@@ -351,23 +357,18 @@
         if step > 0:
             total = send_back()
         take_relayed(half)
-        forward = jnp.zeros((owned * width, part), jnp.float32)
+        forward = [jnp.zeros((width, part), jnp.float32)] * owned
         for k in range(tile_count):
-            vector = stage[cols_ref[k]]
-            spread = []
+            value = jnp.dot(stage[cols_ref[k]], turned[k], preferred_element_type=jnp.float32)
             for i in range(owned):
-                mask = masks[k, i]
-                mask = jnp.concatenate([jnp.concatenate([mask, mask], axis=1)] * (width // 16), axis=0)
-                spread.append(vector * mask)
-            forward = forward + jnp.dot(
-                jnp.concatenate(spread, axis=0), turned[k], preferred_element_type=jnp.float32
-            )
+                mask = jnp.concatenate([masks[k, i]] * (part // 128), axis=1)
+                forward[i] = forward[i] + value * jnp.concatenate([mask] * (width // 8), axis=0)
         for i in range(owned):
-            direct_out[i] = forward[i * width : (i + 1) * width].astype(jnp.bfloat16)
+            direct_out[i] = forward[i].astype(jnp.bfloat16)
         for peer in grp_peers:
             to_grp(peer, direct_out.at[peer], direct_in.at[g], direct_send, direct_recv).start()
         for i in range(owned):
-            total = total + forward[i * width : (i + 1) * width] * jnp.where(g == i, 1.0, 0.0)
+            total = total + forward[i] * jnp.where(g == i, 1.0, 0.0)
         for slot in range(owner_count):
             history[slot, step * width : (step + 1) * width, :] = stage[slot]
         sent_vectors(own_too=step > 0)
@@ -480,7 +481,7 @@
             dma((4,)),
             pltpu.VMEM(matrix.shape, jnp.bfloat16),
             pltpu.VMEM(matrix.shape, jnp.bfloat16),
-            pltpu.VMEM((tile_count, owned, 16, 128), jnp.bfloat16),
+            pltpu.VMEM((tile_count, owned, 8, 128), jnp.float32),
             pltpu.VMEM((tile_count + 1, width, part), jnp.float32),
             pltpu.VMEM((2, owner_count, width, part), jnp.bfloat16),
             pltpu.VMEM((owner_count, width, part), jnp.bfloat16),

time: 70.6 us -> 69 us (0.977)
  Pallas kernels: 69.2 us -> 67.6 us
    pallas_call x1, Pallas kernels: 68.5 us -> 66.9 us  [per_device(): pl.pallas_call(functools.partial(kernel, ITERS, group_count, owner_count)...]
where the time goes in v7:
time: 69 us; the launch traced here: 68.9 us
  Pallas kernels  67.6 us (98%)
  between operations  1.29 us (2%)
    pallas_call x1, Pallas kernels, per_device(): pl.pallas_call(functools.partial(kernel, ITERS, group_count, owner_count)...  66.9 us

profile of v7, /device:TPU:1, one launch (start us, length us, event | category | flops | bytes accessed | tf_op | source)
XLA Modules:
  0.0 68.9 jit_solution(17430355487662023820)
XLA Ops:
  1.3 66.9 %shard_map.85 = (f32[4,32,128]{2,1,0:T(8,128)S(1)}, f32[4,32,32]{2,1,0:T(8,128)S(1)}, f32[32,1024]{1,0:T(8,128)S(1)}) custom-call(f32[32,1024]{1,0:T(8,128)} %start_hbm.1, f32[1,1024]{1,0:T(1,128)} %bitcast.7, s32[32]{0:T(128)} %bitcast.8, s32[32]{0:T(128)} %bitcast.9, s32[1]{0:T(128)} %bitcast.5.live_ref, bf16[32,256,256]{2,1,0:T(8,128)(2,1)} %bitcast.6), custom_call_target="tpu_custom_call" | custom-call | tf_op jit(solution)/shard_map/pallas_call | solution.py:471
  68.2 0.7 %shard_map.86 = (f32[4,32,128]{2,1,0:T(8,128)}, f32[4,32,32]{2,1,0:T(8,128)}, f32[32,1024]{1,0:T(8,128)}) custom-call(f32[4,32,128]{2,1,0:T(8,128)S(1)} %get-tuple-element.6.proj_in, f32[4,32,32]{2,1,0:T(8,128)S(1)} %get-tuple-element.7.fac_in, f32[32,1024]{1,0:T(8,128)S(1)} %get-tuple-element.8.next_in), custom_call_target="tpu_custom_call" | custom-call | tf_op jit(solution)/shard_map/pallas_call | solution.py:511

commit v8 on v7

--- a/solution.py
+++ b/solution.py
@@ -76,9 +76,9 @@
     start_hbm, shift_hbm, rows_hbm, cols_hbm, live_ref, tiles_hbm,
     proj_ref, fac_ref, next_ref,
     start_ref, shift_ref, rows_ref, cols_ref, input_sem, tiles_ref, turned, masks, products, gathered, stage, history, own, own_history, back_out, back_in, direct_out, direct_in,
-    pair_out, pair_in, dots_grp, basis, images, transform, place_vector, place_ref, tile_sem, place_sem,
+    pair_out, pair_in, dots_grp, chip_out, chip_in, basis, images, transform, place_vector, place_ref, tile_sem, place_sem,
     gather_send, gather_recv, relay_send, relay_recv, own_send, own_recv,
-    pair_send, pair_recv, back_send, back_recv, direct_send, direct_recv, dots_send, dots_recv,
+    pair_send, pair_recv, back_send, back_recv, direct_send, direct_recv, dots_send, dots_recv, chip_send, chip_recv,
 ):
     g = lax.axis_index("grp")
     r = lax.axis_index("row")
@@ -138,26 +138,29 @@
 
     others = group_count - 1
 
-    def send_vectors(half, operand, relayed=True, own_too=True):
+    def send_own(operand):
+        own[g] = operand
+        for peer in grp_peers:
+            to_grp(peer, own.at[g], own.at[g], own_send, own_recv).start()
+
+    def send_vectors(half, operand, own_too=True):
         gathered[half, r] = operand
         if own_too:
-            own[g] = operand
-            for peer in grp_peers:
-                to_grp(peer, own.at[g], own.at[g], own_send, own_recv).start()
+            send_own(operand)
         for i, peer in enumerate(targets):
             to_row(
                 peer * 2 + core, gathered.at[half, r], gathered.at[half, r], gather_send, gather_recv.at[half, i]
             ).start()
-        if relayed:
-            to_row(partner, gathered.at[half, r], gathered.at[half, r], gather_send, relay_recv.at[half]).start()
+        to_row(partner, gathered.at[half, r], gathered.at[half, r], gather_send, relay_recv.at[half]).start()
         stage[r] = operand
 
-    def sent_vectors(relayed=True, own_too=True):
-        bulk = gathered.at[0, pl.ds(0, chips if relayed else chips - 1)]
+    def sent_own():
+        bulk = own.at[pl.ds(0, others)]
+        to_grp(grp_peers[0], bulk, bulk, own_send, own_send).wait_send()
+
+    def sent_vectors():
+        bulk = gathered.at[0, pl.ds(0, chips)]
         to_row(partner, bulk, bulk, gather_send, gather_send).wait_send()
-        if own_too:
-            bulk = own.at[pl.ds(0, others)]
-            to_grp(grp_peers[0], bulk, bulk, own_send, own_send).wait_send()
 
     def take_own():
         bulk = own.at[pl.ds(0, others)]
@@ -173,8 +176,7 @@
             slot = peer * 2 + core
             block = gathered.at[half, slot]
             to_row(slot, block, block, gather_send, gather_recv.at[half, i]).wait_recv()
-            if step < steps:
-                to_row(partner, block, block, relay_send, relay_recv.at[half]).start()
+            to_row(partner, block, block, relay_send, relay_recv.at[half]).start()
             stage[slot] = gathered[half, slot]
             batch.append(slot)
             if count % 5 == 4:
@@ -232,17 +234,23 @@
             dots = dots + lax.dot_general(vector, right, NT, preferred_element_type=jnp.float32)
         return dots
 
+    def encode(step, dots):
+        gram, cross = dots
+        high = gram.astype(jnp.bfloat16).astype(jnp.float32)
+        pieces = [high, gram - high]
+        if step > 0:
+            pieces.append(cross)
+        if step % 2 == 1:
+            pieces.append(jnp.zeros((8, 128), jnp.float32))
+        return jnp.concatenate(pieces, axis=0).astype(jnp.bfloat16)
+
+    def pack_both(step, dots):
+        return pack(dots[:, :width]), pack(dots[:, width:]) if step > 0 else None
+
     def send_dots(step, half, dots):
         rows = packed_rows(step)
         me = g * 2 + core
-        gram = pack(dots[:, :width])
-        high = gram.astype(jnp.bfloat16).astype(jnp.float32)
-        dots_grp[half, me, :16] = jnp.concatenate([high, gram - high], axis=0).astype(jnp.bfloat16)
-        if step > 0:
-            cross = pack(dots[:, width:])
-            if step % 2 == 1:
-                cross = jnp.concatenate([cross, jnp.zeros((8, 128), jnp.float32)], axis=0)
-            dots_grp[half, me, 16 : 16 + cross.shape[0]] = cross.astype(jnp.bfloat16)
+        dots_grp[half, me, rows] = encode(step, dots)
         block = dots_grp.at[half, me, rows]
         for peer in grp_peers:
             to_grp(peer, block, block, dots_send, dots_recv.at[half]).start()
@@ -353,7 +361,7 @@
         if step == 0:
             total = send_back()
         dots = take_gathered(step, half)
-        send_dots(step, half, dots)
+        send_dots(step, half, pack_both(step, dots))
         if step > 0:
             total = send_back()
         take_relayed(half)
@@ -371,7 +379,9 @@
             total = total + forward[i] * jnp.where(g == i, 1.0, 0.0)
         for slot in range(owner_count):
             history[slot, step * width : (step + 1) * width, :] = stage[slot]
-        sent_vectors(own_too=step > 0)
+        sent_vectors()
+        if step > 0:
+            sent_own()
         relays_sent()
         cross, gram = take_dots(step, half)
         left, rest = current, None
@@ -396,7 +406,15 @@
             total = total - rest
         image = dot_nn(inverse, total)
         current = image + ahead
-        send_vectors(1 - half, current.astype(jnp.bfloat16), step < steps - 1)
+        if step < steps - 1:
+            send_vectors(1 - half, current.astype(jnp.bfloat16))
+        else:
+            send_own(current.astype(jnp.bfloat16))
+            stage[r] = current.astype(jnp.bfloat16)
+            local = pack_both(steps, slot_dots(steps, [r]))
+            chip_out[...] = encode(steps, local)
+            for i, peer in enumerate(targets):
+                to_row(peer * 2 + core, chip_out, chip_in.at[i], chip_send, chip_recv).start()
         basis[step * width : (step + 1) * width, :] = now
         images[step * width : (step + 1) * width, :] = image
         if step > 0:
@@ -419,11 +437,15 @@
         dots_sent(step, half)
 
     half = steps % 2
-    dots = take_gathered(steps, half)
-    send_dots(steps, half, dots)
     take_own()
     keep_own(steps)
-    sent_vectors(False)
+    sent_own()
+    to_row(partner, chip_in, chip_in, chip_send, chip_recv).wait_recv()
+    summed = chip_in[0].astype(jnp.float32)
+    for i in range(1, chips - 1):
+        summed = summed + chip_in[i].astype(jnp.float32)
+    send_dots(steps, half, (local[0] + summed[:8] + summed[8:16], local[1] + summed[16:]))
+    to_row(partner, chip_in, chip_in, chip_send, chip_recv).wait_send()
     cross, gram = take_dots(steps, half)
     combine = dot_nn(cross, transform[...])
     high = combine.astype(jnp.bfloat16)
@@ -495,6 +517,8 @@
             pltpu.VMEM((pair_count, width, part), jnp.bfloat16),
             pltpu.VMEM((2, pair_count, width, part), jnp.bfloat16),
             pltpu.VMEM((2, 2 * group_count, packed, total_cols), jnp.bfloat16),
+            pltpu.VMEM((packed, total_cols), jnp.bfloat16),
+            pltpu.VMEM((chips - 1, packed, total_cols), jnp.bfloat16),
             pltpu.VMEM((total_cols, part), jnp.float32),
             pltpu.VMEM((total_cols, part), jnp.float32),
             pltpu.VMEM((total_cols, total_cols), jnp.float32),
@@ -502,7 +526,7 @@
             pltpu.SMEM((8, owned * owner_count), jnp.int32),
             dma, dma,
             dma, dma((2, owner_count // 2 - 1)), dma, dma((2,)), dma, dma,
-            dma, dma((2,)), dma, dma((2,)), dma, dma, dma, dma((2,)),
+            dma, dma((2,)), dma, dma((2,)), dma, dma, dma, dma((2,)), dma, dma,
         ],
         compiler_params=pltpu.CompilerParams(
             collective_id=0, has_side_effects=True, vmem_limit_bytes=60 * 1024 * 1024

time: 69 us -> 68.1 us (0.987)
  Pallas kernels: 67.6 us -> 66.7 us
    pallas_call x1, Pallas kernels: 66.9 us -> 66 us  [per_device(): pl.pallas_call(functools.partial(kernel, ITERS, group_count, owner_count)...]
where the time goes in v8:
time: 68.1 us; the launch traced here: 68 us
  Pallas kernels  66.7 us (98%)
  between operations  1.29 us (2%)
    pallas_call x1, Pallas kernels, per_device(): pl.pallas_call(functools.partial(kernel, ITERS, group_count, owner_count)...  66 us

profile of v8, /device:TPU:1, one launch (start us, length us, event | category | flops | bytes accessed | tf_op | source)
XLA Modules:
  0.0 68.0 jit_solution(10443149286118343337)
XLA Ops:
  1.3 66.0 %shard_map.85 = (f32[4,32,128]{2,1,0:T(8,128)S(1)}, f32[4,32,32]{2,1,0:T(8,128)S(1)}, f32[32,1024]{1,0:T(8,128)S(1)}) custom-call(f32[32,1024]{1,0:T(8,128)} %start_hbm.1, f32[1,1024]{1,0:T(1,128)} %bitcast.7, s32[32]{0:T(128)} %bitcast.8, s32[32]{0:T(128)} %bitcast.9, s32[1]{0:T(128)} %bitcast.5.live_ref, bf16[32,256,256]{2,1,0:T(8,128)(2,1)} %bitcast.6), custom_call_target="tpu_custom_call" | custom-call | tf_op jit(solution)/shard_map/pallas_call | solution.py:493
  67.3 0.7 %shard_map.86 = (f32[4,32,128]{2,1,0:T(8,128)}, f32[4,32,32]{2,1,0:T(8,128)}, f32[32,1024]{1,0:T(8,128)}) custom-call(f32[4,32,128]{2,1,0:T(8,128)S(1)} %get-tuple-element.6.proj_in, f32[4,32,32]{2,1,0:T(8,128)S(1)} %get-tuple-element.7.fac_in, f32[32,1024]{1,0:T(8,128)S(1)} %get-tuple-element.8.next_in), custom_call_target="tpu_custom_call" | custom-call | tf_op jit(solution)/shard_map/pallas_call | solution.py:535

commit v9 on v8

--- a/solution.py
+++ b/solution.py
@@ -241,7 +241,8 @@
         if step > 0:
             pieces.append(cross)
         if step % 2 == 1:
-            pieces.append(jnp.zeros((8, 128), jnp.float32))
+            newest = cross[cross.shape[0] - 8 :]
+            pieces.append(newest - newest.astype(jnp.bfloat16).astype(jnp.float32))
         return jnp.concatenate(pieces, axis=0).astype(jnp.bfloat16)
 
     def pack_both(step, dots):
@@ -270,7 +271,11 @@
         gram = unpack(summed[:8] + summed[8:16], width)[0]
         if step == 0:
             return None, gram
-        pieces = unpack(summed[16:], step * width)
+        old = summed[16 : 16 + step * 8]
+        if step % 2 == 1:
+            newest = old[step * 8 - 8 :] + summed[16 + step * 8 :]
+            old = newest if step == 1 else jnp.concatenate([old[: step * 8 - 8], newest], axis=0)
+        pieces = unpack(old, step * width)
         whole = jnp.concatenate(pieces, axis=1) if len(pieces) > 1 else pieces[0]
         cross = dot_nt(whole, transform[:, : step * width])
         return cross, gram - dot_nt(cross, cross)
@@ -321,7 +326,7 @@
             turned[j * 4 + i] = tiles_ref[j * 4 + i].T
         return carry
 
-    coef = None
+    coef, middle = None, MIDDLE
     lane = lax.broadcasted_iota(jnp.int32, (width, total_cols), 1)
     sub = lax.broadcasted_iota(jnp.int32, (width, total_cols), 0)
     for step in range(steps):
@@ -388,9 +393,12 @@
         if step > 0:
             left = left - dot_nn(cross, basis[...])
             rest = dot_nn(cross, images[...])
+            first = cross + coef
+            newest = jnp.where(lane == (step - 1) * width + sub, first, 0.0)
+            middle = -jnp.sum(newest, axis=(0, 1), keepdims=True) / width
         upper, inverse = factor_and_inverse(gram)
         now = dot_nn(inverse, left)
-        ahead = now * (MIDDLE - shift)
+        ahead = now * (middle - shift)
         if step > 0:
             ahead = ahead - dot_nn(upper, basis[(step - 1) * width : step * width, :])
         bulk = back_in.at[half, pl.ds(0, chips - 1 + far)]
@@ -418,7 +426,7 @@
         basis[step * width : (step + 1) * width, :] = now
         images[step * width : (step + 1) * width, :] = image
         if step > 0:
-            proj_ref[step - 1] = cross + coef
+            proj_ref[step - 1] = first
             fac_ref[step - 1] = upper.T
         unit = jnp.where(lane == step * width + sub, 1.0, 0.0)
         if step == 0:
@@ -427,7 +435,7 @@
         else:
             transform[step * width : (step + 1) * width, :] = dot_nn(inverse, unit - dot_nn(cross, transform[...]))
             wide = jnp.concatenate([upper] * (total_cols // width), axis=1)
-            coef = -MIDDLE * unit + jnp.where((lane >= (step - 1) * width) & (lane < step * width), wide, 0.0)
+            coef = -middle * unit + jnp.where((lane >= (step - 1) * width) & (lane < step * width), wide, 0.0)
         bulk = pair_out.at[near_rows]
         to_row(partner, bulk, bulk, pair_send, pair_recv.at[half]).wait_send()
         bulk = back_out.at[pl.ds(0, chips - 1 + far)]

time: 68.1 us -> 68.2 us (level)
  no operation moved by 1% of the time
where the time goes in v9:
time: 68.2 us; the launch traced here: 68 us
  Pallas kernels  66.8 us (98%)
  between operations  1.29 us (2%)
    pallas_call x1, Pallas kernels, per_device(): pl.pallas_call(functools.partial(kernel, ITERS, group_count, owner_count)...  66 us

profile of v9, /device:TPU:1, one launch (start us, length us, event | category | flops | bytes accessed | tf_op | source)
XLA Modules:
  0.0 68.0 jit_solution(10157791905580078684)
XLA Ops:
  1.3 66.0 %shard_map.85 = (f32[4,32,128]{2,1,0:T(8,128)S(1)}, f32[4,32,32]{2,1,0:T(8,128)S(1)}, f32[32,1024]{1,0:T(8,128)S(1)}) custom-call(f32[32,1024]{1,0:T(8,128)} %start_hbm.1, f32[1,1024]{1,0:T(1,128)} %bitcast.7, s32[32]{0:T(128)} %bitcast.8, s32[32]{0:T(128)} %bitcast.9, s32[1]{0:T(128)} %bitcast.5.live_ref, bf16[32,256,256]{2,1,0:T(8,128)(2,1)} %bitcast.6), custom_call_target="tpu_custom_call" | custom-call | tf_op jit(solution)/shard_map/pallas_call | solution.py:501
  67.3 0.7 %shard_map.86 = (f32[4,32,128]{2,1,0:T(8,128)}, f32[4,32,32]{2,1,0:T(8,128)}, f32[32,1024]{1,0:T(8,128)}) custom-call(f32[4,32,128]{2,1,0:T(8,128)S(1)} %get-tuple-element.6.proj_in, f32[4,32,32]{2,1,0:T(8,128)S(1)} %get-tuple-element.7.fac_in, f32[32,1024]{1,0:T(8,128)S(1)} %get-tuple-element.8.next_in), custom_call_target="tpu_custom_call" | custom-call | tf_op jit(solution)/shard_map/pallas_call | solution.py:543

commit v10 on v9

--- a/solution.py
+++ b/solution.py
@@ -68,7 +68,7 @@
 
 
 def far_first(chips):
-    return sorted(range(1, chips), key=lambda d: -away(d, chips))
+    return sorted(range(1, chips), key=lambda d: (-away(d, chips), -min(d // SIDE, 4 - d // SIDE)))
 
 
 def kernel(
@@ -172,7 +172,7 @@
 
     def take_gathered(step, half):
         dots, batch = None, [r]
-        for count, (i, peer) in enumerate(reversed(list(enumerate(sources)))):
+        for count, (i, peer) in enumerate(list(enumerate(sources))):
             slot = peer * 2 + core
             block = gathered.at[half, slot]
             to_row(slot, block, block, gather_send, gather_recv.at[half, i]).wait_recv()

time: 68.2 us -> 67.4 us (0.988)
  Pallas kernels: 66.8 us -> 66 us
    pallas_call x1, Pallas kernels: 66 us -> 65.3 us  [per_device(): pl.pallas_call(functools.partial(kernel, ITERS, group_count, owner_count)...]
where the time goes in v10:
time: 67.4 us; the launch traced here: 67.3 us
  Pallas kernels  66 us (98%)
  between operations  1.29 us (2%)
    pallas_call x1, Pallas kernels, per_device(): pl.pallas_call(functools.partial(kernel, ITERS, group_count, owner_count)...  65.3 us

profile of v10, /device:TPU:1, one launch (start us, length us, event | category | flops | bytes accessed | tf_op | source)
XLA Modules:
  0.0 67.3 jit_solution(13804371412007200708)
XLA Ops:
  1.3 65.3 %shard_map.85 = (f32[4,32,128]{2,1,0:T(8,128)S(1)}, f32[4,32,32]{2,1,0:T(8,128)S(1)}, f32[32,1024]{1,0:T(8,128)S(1)}) custom-call(f32[32,1024]{1,0:T(8,128)} %start_hbm.1, f32[1,1024]{1,0:T(1,128)} %bitcast.7, s32[32]{0:T(128)} %bitcast.8, s32[32]{0:T(128)} %bitcast.9, s32[1]{0:T(128)} %bitcast.5.live_ref, bf16[32,256,256]{2,1,0:T(8,128)(2,1)} %bitcast.6), custom_call_target="tpu_custom_call" | custom-call | tf_op jit(solution)/shard_map/pallas_call | solution.py:501
  66.5 0.7 %shard_map.86 = (f32[4,32,128]{2,1,0:T(8,128)}, f32[4,32,32]{2,1,0:T(8,128)}, f32[32,1024]{1,0:T(8,128)}) custom-call(f32[4,32,128]{2,1,0:T(8,128)S(1)} %get-tuple-element.6.proj_in, f32[4,32,32]{2,1,0:T(8,128)S(1)} %get-tuple-element.7.fac_in, f32[32,1024]{1,0:T(8,128)S(1)} %get-tuple-element.8.next_in), custom_call_target="tpu_custom_call" | custom-call | tf_op jit(solution)/shard_map/pallas_call | solution.py:543

commit v11 on v10

--- a/solution.py
+++ b/solution.py
@@ -9,7 +9,6 @@
 
 ITERS = 4
 MESH = pl.DeviceIdType.MESH
-HIGH = lax.Precision.HIGHEST
 NT = (((1,), (1,)), ((), ()))
 MIDDLE = 1.25
 PANEL = 16
@@ -17,12 +16,26 @@
 NEAR = 2
 
 
+def halves(x):
+    high = x.astype(jnp.bfloat16)
+    return high, (x - high.astype(jnp.float32)).astype(jnp.bfloat16)
+
+
+def dot_split(a, b, dims):
+    (a_high, a_low), (b_high, b_low) = halves(a), halves(b)
+
+    def dot(x, y):
+        return lax.dot_general(x, y, dims, preferred_element_type=jnp.float32)
+
+    return dot(a_high, b_low) + dot(a_low, b_high) + dot(a_high, b_high)
+
+
 def dot_nt(a, b):
-    return lax.dot_general(a, b, NT, precision=HIGH, preferred_element_type=jnp.float32)
+    return dot_split(a, b, NT)
 
 
 def dot_nn(a, b):
-    return jnp.dot(a, b, precision=HIGH, preferred_element_type=jnp.float32)
+    return dot_split(a, b, (((1,), (0,)), ((), ())))
 
 
 def factor_and_inverse(gram):

time: 67.4 us -> 67.1 us (level)
  no operation moved by 1% of the time
where the time goes in v11:
time: 67.1 us; the launch traced here: 67 us
  Pallas kernels  65.7 us (98%)
  between operations  1.29 us (2%)
    pallas_call x1, Pallas kernels, per_device(): pl.pallas_call(functools.partial(kernel, ITERS, group_count, owner_count)...  65 us

profile of v11, /device:TPU:1, one launch (start us, length us, event | category | flops | bytes accessed | tf_op | source)
XLA Modules:
  0.0 67.0 jit_solution(4226396746254534041)
XLA Ops:
  1.3 65.0 %shard_map.85 = (f32[4,32,128]{2,1,0:T(8,128)S(1)}, f32[4,32,32]{2,1,0:T(8,128)S(1)}, f32[32,1024]{1,0:T(8,128)S(1)}) custom-call(f32[32,1024]{1,0:T(8,128)} %start_hbm.1, f32[1,1024]{1,0:T(1,128)} %bitcast.7, s32[32]{0:T(128)} %bitcast.8, s32[32]{0:T(128)} %bitcast.9, s32[1]{0:T(128)} %bitcast.5.live_ref, bf16[32,256,256]{2,1,0:T(8,128)(2,1)} %bitcast.6), custom_call_target="tpu_custom_call" | custom-call | tf_op jit(solution)/shard_map/pallas_call | solution.py:514
  66.3 0.7 %shard_map.86 = (f32[4,32,128]{2,1,0:T(8,128)}, f32[4,32,32]{2,1,0:T(8,128)}, f32[32,1024]{1,0:T(8,128)}) custom-call(f32[4,32,128]{2,1,0:T(8,128)S(1)} %get-tuple-element.6.proj_in, f32[4,32,32]{2,1,0:T(8,128)S(1)} %get-tuple-element.7.fac_in, f32[32,1024]{1,0:T(8,128)S(1)} %get-tuple-element.8.next_in), custom_call_target="tpu_custom_call" | custom-call | tf_op jit(solution)/shard_map/pallas_call | solution.py:556

commit v12 on v11

--- a/solution.py
+++ b/solution.py
@@ -11,7 +11,7 @@
 MESH = pl.DeviceIdType.MESH
 NT = (((1,), (1,)), ((), ()))
 MIDDLE = 1.25
-PANEL = 16
+PANEL = 32
 SIDE = 4
 NEAR = 2
 

time: 67.1 us -> 67.7 us (level)
  no operation moved by 1% of the time
where the time goes in v12:
time: 67.7 us; the launch traced here: 67.6 us
  Pallas kernels  66.3 us (98%)
  between operations  1.29 us (2%)
    pallas_call x1, Pallas kernels, per_device(): pl.pallas_call(functools.partial(kernel, ITERS, group_count, owner_count)...  65.6 us

profile of v12, /device:TPU:1, one launch (start us, length us, event | category | flops | bytes accessed | tf_op | source)
XLA Modules:
  0.0 67.6 jit_solution(3861599392205423437)
XLA Ops:
  1.3 65.6 %shard_map.85 = (f32[4,32,128]{2,1,0:T(8,128)S(1)}, f32[4,32,32]{2,1,0:T(8,128)S(1)}, f32[32,1024]{1,0:T(8,128)S(1)}) custom-call(f32[32,1024]{1,0:T(8,128)} %start_hbm.1, f32[1,1024]{1,0:T(1,128)} %bitcast.7, s32[32]{0:T(128)} %bitcast.8, s32[32]{0:T(128)} %bitcast.9, s32[1]{0:T(128)} %bitcast.5.live_ref, bf16[32,256,256]{2,1,0:T(8,128)(2,1)} %bitcast.6), custom_call_target="tpu_custom_call" | custom-call | tf_op jit(solution)/shard_map/pallas_call | solution.py:514
  66.9 0.7 %shard_map.86 = (f32[4,32,128]{2,1,0:T(8,128)}, f32[4,32,32]{2,1,0:T(8,128)}, f32[32,1024]{1,0:T(8,128)}) custom-call(f32[4,32,128]{2,1,0:T(8,128)S(1)} %get-tuple-element.6.proj_in, f32[4,32,32]{2,1,0:T(8,128)S(1)} %get-tuple-element.7.fac_in, f32[32,1024]{1,0:T(8,128)S(1)} %get-tuple-element.8.next_in), custom_call_target="tpu_custom_call" | custom-call | tf_op jit(solution)/shard_map/pallas_call | solution.py:556
